TPU v7x, 256 devices: a whole 4x4x8 slice. The times are simulated.
256 devices in a mesh: ep: 8 (over x, core), fsdp: 32 (over z, y).
Axes of the slice: x: 4, y: 4, z: 8, core: 2. Of those that a mesh axis runs over, the one named last changes fastest.
Arguments:
- train_gate: float32 [128, 2048, 768], P('ep', 'fsdp'), may hold values from -0.25 to 0.25
- other_gate: bfloat16 [128, 2048, 768], P('ep', 'fsdp'), may hold values from -0.0625 to 0.0625
- train_up: float32 [128, 2048, 768], P('ep', 'fsdp'), may hold values from -0.25 to 0.25
- other_up: bfloat16 [128, 2048, 768], P('ep', 'fsdp'), may hold values from -0.0625 to 0.0625
- router_weight: float32 [2048, 128], P('fsdp', 'ep'), may hold values from -0.125 to 0.125
- router_gain: float32 [2048], P('fsdp'), may hold values from 0.25 to 1.75
Outputs:
- ready_gate: bfloat16 [128, 2048, 768], P('ep', None, 'fsdp')
- ready_up: bfloat16 [128, 2048, 768], P('ep', None, 'fsdp')
- scale_gate: float32 [128, 768], P('ep', 'fsdp')
- scale_up: float32 [128, 768], P('ep', 'fsdp')
- serve_router: bfloat16 [2048, 128], replicated
All inputs are finite; a program needn't handle non-finite values. Where the computation divides by a largest or mean magnitude, that divisor is 1e-20 or more.
Results may differ from a plain program's by a relative error of at most 0.001.
Values may be sent and summed in bfloat16 or wider, within the bound.
No kernel may reach another device: no remote copies, remote signals or barrier semaphores. Data moves between devices by JAX's collectives and lax.ppermute only.
A program may use at most 128 MiB of HBM per device.

v0:
```python
import jax
import jax.numpy as jnp
from jax import lax
from jax.sharding import PartitionSpec as P

D_MODEL = 2048


def in_blocks(shard, dim, devices):
    before, after = (shard.shape[:dim], shard.shape[dim + 1 :])
    return jnp.moveaxis(shard.reshape(*before, devices, -1, *after), dim, 0)


def summed_on_arrival(shard, axis, dim):
    pieces = in_blocks(shard, dim, lax.axis_size(axis))
    arrived = lax.all_to_all(pieces, axis, split_axis=0, concat_axis=0, tiled=True)
    return arrived.sum(axis=0)


def rows_for(lines, devices):
    spare = -lines.shape[0] % devices
    if not spare:
        return lines
    return jnp.concatenate([lines, jnp.zeros((spare, *lines.shape[1:]), lines.dtype)])


def sent_to_all(shard, axis):
    copies = jnp.broadcast_to(shard, (lax.axis_size(axis), *shard.shape))
    return lax.all_to_all(copies, axis, split_axis=0, concat_axis=0, tiled=True)


def joined_along(pieces, dim):
    pieces = jnp.moveaxis(pieces, 0, dim)
    dims = pieces.shape
    return pieces.reshape(*dims[:dim], dims[dim] * dims[dim + 1], *dims[dim + 2 :])


def collect(shard, axis, dim):
    pieces = sent_to_all(shard, axis)
    return joined_along(pieces, dim)


def nested_sum(shard, axes):
    own = summed_on_arrival(rows_for(shard, lax.axis_size(axes)), axes, 0)
    whole = collect(own, axes, 0)
    return whole[: len(shard)].reshape(shard.shape)


def in_one(arrays, axis):
    ends = [0]
    for a in arrays:
        ends.append(ends[-1] + a.size)
    total = nested_sum(jnp.concatenate([a.ravel() for a in arrays]), axis)
    return tuple((total[b:e].reshape(a.shape) for a, b, e in zip(arrays, ends, ends[1:])))


def in_one_piece(arrays, axis, split_dim, concat_dim, along):
    both = jnp.concatenate(arrays, axis=along)
    filled, at, outs = (
        lax.all_to_all(both, axis, split_axis=split_dim, concat_axis=concat_dim, tiled=True),
        0,
        [],
    )
    for a in arrays:
        outs.append(lax.slice_in_dim(filled, at, at + a.shape[along], axis=along))
        at += a.shape[along]
    return tuple(outs)


def per_device(train_gate, other_gate, train_up, other_up, router_weight, router_gain):
    latest_gate = train_gate + other_gate.astype(jnp.float32)
    latest_up = train_up + other_up.astype(jnp.float32)
    total_gate, total_up = in_one(
        (jnp.sum(jnp.abs(latest_gate), axis=1), jnp.sum(jnp.abs(latest_up), axis=1)), "fsdp"
    )
    scale_gate = total_gate / D_MODEL
    scale_up = total_up / D_MODEL
    narrow_gate, narrow_up = (
        (latest_gate / jnp.expand_dims(scale_gate, 1)).astype(jnp.bfloat16),
        (latest_up / jnp.expand_dims(scale_up, 1)).astype(jnp.bfloat16),
    )
    ready_gate, ready_up = in_one_piece((narrow_gate, narrow_up), "fsdp", 2, 1, 0)
    scale_gate = lax.dynamic_slice_in_dim(
        scale_gate, lax.axis_index("fsdp") * ready_gate.shape[2], ready_gate.shape[2], axis=1
    )
    scale_up = lax.dynamic_slice_in_dim(
        scale_up, lax.axis_index("fsdp") * ready_up.shape[2], ready_up.shape[2], axis=1
    )
    part_router = (router_weight * router_gain[:, None]).astype(jnp.bfloat16)
    row_router = collect(part_router, "fsdp", 0)
    serve_router = collect(row_router, "ep", 1)
    return (ready_gate, ready_up, scale_gate, scale_up, serve_router)


def solution(mesh):
    in_specs = (
        P("ep", "fsdp", None),
        P("ep", "fsdp", None),
        P("ep", "fsdp", None),
        P("ep", "fsdp", None),
        P("fsdp", "ep"),
        P("fsdp"),
    )
    out_specs = (
        P("ep", None, "fsdp"),
        P("ep", None, "fsdp"),
        P("ep", "fsdp"),
        P("ep", "fsdp"),
        P(),
    )
    return jax.shard_map(
        per_device, mesh=mesh, in_specs=in_specs, out_specs=out_specs, check_vma=False
    )
```

profile of v0, /device:TPU:22, one launch (start us, length us, event | category | flops | bytes accessed | tf_op | source)
XLA Modules:
  0.0 184.5 jit_solution(4321875184413346923)
XLA Ops:
  0.6 0.0 copy-start.4
  0.6 0.0 copy-start.5
  0.7 4.9 %abs_reduce_fusion = (f32[16,768]{1,0:T(8,128)S(1)}, f32[16,768]{1,0:T(8,128)S(1)}) fusion(f32[16,64,768]{2,1,0:T(8,128)} %param.8, bf16[16,64,768]{2,1,0:T(8,128)(2,1)} %param.9, f32[16,64,768]{2,1,0:T(8,128)} %param.6, bf16[16,64,768]{2,1,0:T(8,128)(2,1)} %param.7), kind=kLoop, calls=%fused_computation.3 | loop fusion | flops 6266880 | bytes 9535488 | tf_op jit(solution)/shard_map/reduce_sum | solution.py:74
  5.6 0.0 copy-start
  5.6 0.7 all_to_all.27
  6.3 11.7 %all-to-all-start = ((f32[32,1,768]{2,1,0:T(1,128)}), f32[32,1,768]{2,1,0:T(1,128)S(1)}, u32[]{:S(2)}, u32[]{:S(2)}) async-start(f32[32,1,768]{2,1,0:T(1,128)} %all_to_all.27), calls=%async_computation | async-start | bytes 196608 | tf_op jit(solution)/shard_map/all_to_all | solution.py:16
  18.0 0.0 copy-done.4
  18.0 0.0 copy-done.5
  18.1 0.8 reshape.53
  18.9 7.4 %all-to-all-done = f32[32,1,768]{2,1,0:T(1,128)S(1)} async-done(((f32[32,1,768]{2,1,0:T(1,128)}), f32[32,1,768]{2,1,0:T(1,128)S(1)}, u32[]{:S(2)}, u32[]{:S(2)}) %all-to-all-start) | async-done | bytes 98336 | tf_op jit(solution)/shard_map/all_to_all | solution.py:16
  26.2 5.8 %all-to-all-start.3 = ((bf16[32,2,512]{2,1,0:T(2,128)(2,1)}), bf16[32,2,512]{2,1,0:T(2,128)(2,1)S(1)}, u32[]{:S(2)}, u32[]{:S(2)}) async-start(bf16[32,2,512]{2,1,0:T(2,128)(2,1)} %reshape.53), calls=%async_computation.3 | async-start | bytes 131072 | tf_op jit(solution)/shard_map/all_to_all | solution.py:29
  32.0 0.1 reduce_sum.29
  32.1 8.0 %all-to-all-done.3 = bf16[32,2,512]{2,1,0:T(2,128)(2,1)S(1)} async-done(((bf16[32,2,512]{2,1,0:T(2,128)(2,1)}), bf16[32,2,512]{2,1,0:T(2,128)(2,1)S(1)}, u32[]{:S(2)}, u32[]{:S(2)}) %all-to-all-start.3) | async-done | bytes 65568 | tf_op jit(solution)/shard_map/all_to_all | solution.py:29
  40.1 0.0 copy-start.3
  40.1 0.7 broadcast_in_dim.12
  40.8 0.0 copy-done.3
  40.8 5.8 %all-to-all-start.1 = ((f32[32,1,768]{2,1,0:T(1,128)}), f32[32,1,768]{2,1,0:T(1,128)S(1)}, u32[]{:S(2)}, u32[]{:S(2)}) async-start(f32[32,1,768]{2,1,0:T(1,128)} %broadcast_in_dim.12), calls=%async_computation.1 | async-start | bytes 196608 | tf_op jit(solution)/shard_map/all_to_all | solution.py:29
  46.6 1.0 reshape.54
  47.7 0.2 reshape.49
  47.8 7.1 %all-to-all-done.1 = f32[32,1,768]{2,1,0:T(1,128)S(1)} async-done(((f32[32,1,768]{2,1,0:T(1,128)}), f32[32,1,768]{2,1,0:T(1,128)S(1)}, u32[]{:S(2)}, u32[]{:S(2)}) %all-to-all-start.1) | async-done | bytes 98336 | tf_op jit(solution)/shard_map/all_to_all | solution.py:29
  54.9 0.8 broadcast_in_dim.14
  55.8 4.8 %all-to-all-start.4 = ((bf16[8,2048,16]{1,2,0:T(8,128)(2,1)}), bf16[8,2048,16]{1,2,0:T(8,128)(2,1)}, u32[]{:S(2)}, u32[]{:S(2)}) async-start(bf16[8,2048,16]{1,2,0:T(8,128)(2,1)} %broadcast_in_dim.14), calls=%async_computation.4 | async-start | bytes 1048576 | tf_op jit(solution)/shard_map/all_to_all | solution.py:29
  60.5 0.1 slice_multiply_fusion.1
  60.7 0.0 copy-done
  60.7 0.0 copy-start.1
  60.7 0.0 copy-start.2
  60.7 2.0 %divide_convert_fusion = bf16[16,64,768]{2,1,0:T(8,128)(2,1)S(1)} fusion(f32[16,64,768]{2,1,0:T(8,128)S(1)} %copy-done, bf16[16,64,768]{2,1,0:T(8,128)(2,1)} %param.9, f32[16,768]{1,0:T(8,128)S(1)} %bitcast.33), kind=kLoop, calls=%fused_computation.1 | loop fusion | flops 3145728 | bytes 6340608 | tf_op jit(solution)/shard_map/convert_element_type | solution.py:80
  62.8 0.3 copy-done.1
  63.0 0.5 copy-done.2
  63.5 0.5 divide_convert_fusion.1
  64.0 0.3 pad_maximum_fusion
  64.3 9.5 %copy.75 = bf16[32,64,768]{1,0,2:T(8,128)(2,1)} copy(bf16[32,64,768]{2,1,0:T(8,128)(2,1)S(1)} %pad_maximum_fusion) | data formatting | bytes 6291456 | tf_op jit(solution)/shard_map/concatenate | solution.py:58
  73.7 8.8 %reshape.51 = bf16[32,2,24576]{2,1,0:T(2,128)(2,1)} reshape(bf16[768,32,64]{2,1,0:T(8,128)(2,1)} %bitcast.30) | data formatting | bytes 6291456
  82.5 0.0 all-to-all-done.4
  82.5 6.0 %all-to-all-start.2 = ((bf16[32,2,24576]{2,1,0:T(2,128)(2,1)}), bf16[32,2,24576]{2,1,0:T(2,128)(2,1)S(1)}, u32[]{:S(2)}, u32[]{:S(2)}) async-start(bf16[32,2,24576]{2,1,0:T(2,128)(2,1)} %reshape.51), calls=%async_computation.2 | async-start | bytes 6291456 | tf_op jit(solution)/shard_map/all_to_all | solution.py:60
  88.6 0.7 constant_dynamic-slice_fusion.1
  89.3 0.7 constant_dynamic-slice_fusion
  90.0 2.0 %copy.80 = bf16[2048,128]{1,0:T(8,128)(2,1)} copy(bf16[2048,128]{0,1:T(8,128)(2,1)} %bitcast.6) | data formatting | bytes 1048576
  92.0 68.3 %all-to-all-done.2 = bf16[32,2,24576]{2,1,0:T(2,128)(2,1)S(1)} async-done(((bf16[32,2,24576]{2,1,0:T(2,128)(2,1)}), bf16[32,2,24576]{2,1,0:T(2,128)(2,1)S(1)}, u32[]{:S(2)}, u32[]{:S(2)}) %all-to-all-start.2) | async-done | bytes 3145760 | tf_op jit(solution)/shard_map/all_to_all | solution.py:60
  160.3 6.2 %reshape.52 = bf16[768,32,64]{2,1,0:T(8,128)(2,1)} reshape(bf16[32,2,24576]{2,1,0:T(2,128)(2,1)S(1)} %all-to-all-done.2) | data formatting | bytes 6291456
  166.4 5.2 %copy.76 = bf16[32,64,768]{1,2,0:T(8,128)(2,1)S(1)} copy(bf16[32,64,768]{1,0,2:T(8,128)(2,1)} %bitcast.31) | data formatting | bytes 6291456 | tf_op jit(solution)/shard_map/all_to_all | solution.py:60
  171.6 2.7 %fusion = (bf16[16,32,64,24]{2,3,1,0:T(8,128)(2,1)}, bf16[16,32,64,24]{2,3,1,0:T(8,128)(2,1)S(1)}) fusion(bf16[32,32,64,24]{2,3,1,0:T(8,128)(2,1)S(1)} %bitcast.29), kind=kLoop, calls=%fused_computation.15 | loop fusion | bytes 6291456 | tf_op jit(solution)/shard_map/slice | solution.py:65
  174.4 0.8 copy.77
  175.1 3.4 %slice.25 = bf16[16,2048,24]{1,2,0:T(8,128)(2,1)} reshape(bf16[16,32,64,24]{2,1,3,0:T(8,128)(2,1)S(1)} %copy.77) | data formatting | bytes 3145728 | tf_op jit(solution)/shard_map/slice | solution.py:65
  178.5 2.6 %copy.78 = bf16[16,32,64,24]{2,1,3,0:T(8,128)(2,1)S(1)} copy(bf16[16,32,64,24]{2,3,1,0:T(8,128)(2,1)} %get-tuple-element.40) | data formatting | bytes 3145728 | tf_op jit(solution)/shard_map/slice | solution.py:65
  181.1 3.4 %slice.27 = bf16[16,2048,24]{1,2,0:T(8,128)(2,1)} reshape(bf16[16,32,64,24]{2,1,3,0:T(8,128)(2,1)S(1)} %copy.78) | data formatting | bytes 3145728 | tf_op jit(solution)/shard_map/slice | solution.py:65
  (6 shorter events, 0.1 us)
Async XLA Ops:
  0.6 17.4 %copy-start.4 = (f32[64,16]{0,1:T(8,128)S(1)}, f32[64,16]{0,1:T(8,128)}, u32[]{:S(2)}) copy-start(f32[64,16]{0,1:T(8,128)} %param.10) | copy-start | bytes 12292
  0.6 17.4 %copy-start.5 = (f32[64]{0:T(128)S(1)}, f32[64]{0:T(128)}, u32[]{:S(2)}) copy-start(f32[64]{0:T(128)} %param.11) | copy-start | bytes 772
  5.6 55.1 %copy-start = (f32[16,64,768]{2,1,0:T(8,128)S(1)}, f32[16,64,768]{2,1,0:T(8,128)}, u32[]{:S(2)}) copy-start(f32[16,64,768]{2,1,0:T(8,128)} %param.8) | copy-start | bytes 9437188
  6.3 19.9 %all-to-all-start = ((f32[32,1,768]{2,1,0:T(1,128)}), f32[32,1,768]{2,1,0:T(1,128)S(1)}, u32[]{:S(2)}, u32[]{:S(2)}) async-start(f32[32,1,768]{2,1,0:T(1,128)} %all_to_all.27), calls=%async_computation | async-start | bytes 196608 | tf_op jit(solution)/shard_map/all_to_all | solution.py:16
  26.2 13.9 %all-to-all-start.3 = ((bf16[32,2,512]{2,1,0:T(2,128)(2,1)}), bf16[32,2,512]{2,1,0:T(2,128)(2,1)S(1)}, u32[]{:S(2)}, u32[]{:S(2)}) async-start(bf16[32,2,512]{2,1,0:T(2,128)(2,1)} %reshape.53), calls=%async_computation.3 | async-start | bytes 131072 | tf_op jit(solution)/shard_map/all_to_all | solution.py:29
  40.1 0.7 copy-start.3
  40.8 14.1 %all-to-all-start.1 = ((f32[32,1,768]{2,1,0:T(1,128)}), f32[32,1,768]{2,1,0:T(1,128)S(1)}, u32[]{:S(2)}, u32[]{:S(2)}) async-start(f32[32,1,768]{2,1,0:T(1,128)} %broadcast_in_dim.12), calls=%async_computation.1 | async-start | bytes 196608 | tf_op jit(solution)/shard_map/all_to_all | solution.py:29
  55.8 26.8 %all-to-all-start.4 = ((bf16[8,2048,16]{1,2,0:T(8,128)(2,1)}), bf16[8,2048,16]{1,2,0:T(8,128)(2,1)}, u32[]{:S(2)}, u32[]{:S(2)}) async-start(bf16[8,2048,16]{1,2,0:T(8,128)(2,1)} %broadcast_in_dim.14), calls=%async_computation.4 | async-start | bytes 1048576 | tf_op jit(solution)/shard_map/all_to_all | solution.py:29
  60.7 2.4 %copy-start.1 = (f32[16,64,768]{2,1,0:T(8,128)S(1)}, f32[16,64,768]{2,1,0:T(8,128)}, u32[]{:S(2)}) copy-start(f32[16,64,768]{2,1,0:T(8,128)} %param.6) | copy-start | bytes 9437188
  60.7 2.8 %copy-start.2 = (bf16[16,64,768]{2,1,0:T(8,128)(2,1)S(1)}, bf16[16,64,768]{2,1,0:T(8,128)(2,1)}, u32[]{:S(2)}) copy-start(bf16[16,64,768]{2,1,0:T(8,128)(2,1)} %param.7) | copy-start | bytes 4718596
  82.5 77.7 %all-to-all-start.2 = ((bf16[32,2,24576]{2,1,0:T(2,128)(2,1)}), bf16[32,2,24576]{2,1,0:T(2,128)(2,1)S(1)}, u32[]{:S(2)}, u32[]{:S(2)}) async-start(bf16[32,2,24576]{2,1,0:T(2,128)(2,1)} %reshape.51), calls=%async_computation.2 | async-start | bytes 6291456 | tf_op jit(solution)/shard_map/all_to_all | solution.py:60
where the time goes:
time: 188 us; the launch traced here: 185 us
  waiting for transfers between devices  90.7 us (48%)
  local copies, waits for them, and re-layouts  51 us (27%)
  starting transfers between devices  34.1 us (18%)
  other arithmetic  7.89 us (4%)
    all_to_all x1, waiting for transfers between devices, in_one_piece(): lax.all_to_all(both, axis, split_axis=split_dim, concat_axis=concat_dim,...  68.3 us
    unnamed x20, local copies, waits for them, and re-layouts  19.6 us
    all_to_all x3, starting transfers between devices, sent_to_all(): return lax.all_to_all(copies, axis, split_axis=0, concat_axis=0, tiled=True)  16.3 us
    all_to_all x3, waiting for transfers between devices, sent_to_all(): return lax.all_to_all(copies, axis, split_axis=0, concat_axis=0, tiled=True)  15.1 us
    slice x5, local copies, waits for them, and re-layouts, in_one_piece(): outs.append(lax.slice_in_dim(filled, at, at + a.shape[along], axis=along))  12.9 us
    all_to_all x1, starting transfers between devices, summed_on_arrival(): lax.all_to_all(pieces, axis, split_axis=0, concat_axis=0, tiled=True)  11.7 us
    concatenate x1, local copies, waits for them, and re-layouts, in_one_piece(): both = jnp.concatenate(arrays, axis=along)  9.47 us
    all_to_all x1, waiting for transfers between devices, summed_on_arrival(): lax.all_to_all(pieces, axis, split_axis=0, concat_axis=0, tiled=True)  7.38 us
  transfers between devices with their start and end apart: 5, of which 4 were waited for; matrix products, arithmetic and copies ran while one was open for 14% of the time, Pallas kernels for 0%

commit v1 on v0

v1 whole, which is shorter than its diff:
```python
import functools

import jax
import jax.numpy as jnp
from jax import lax
from jax.experimental import pallas as pl
from jax.experimental.pallas import tpu as pltpu
from jax.sharding import PartitionSpec as P

POWER = 15
SPREAD = 5.0
LEAST = 1e-30
PAIR = 2


def coded(latest):
    mean = jnp.sum(jnp.abs(latest), axis=0, keepdims=True) * (1.0 / (latest.shape[0] * SPREAD))
    norm = jnp.maximum(mean, LEAST).astype(jnp.bfloat16).astype(jnp.float32)
    v = latest * (1.0 / norm)
    v2 = v * v
    v4 = v2 * v2
    v8 = v4 * v4
    return (v8 * v4) * (v2 * v), norm


def encode_kernel(parts, tg, og, tu, ou, out, codes, norms, norm_rows, sems, norm_sem):
    step = pl.program_id(0)
    steps = pl.num_programs(0)
    width = tg.shape[2] // parts
    rows = PAIR * width
    slot = lax.rem(step, 2)

    def copy(s, at):
        return pltpu.make_async_copy(
            codes.at[at], out.at[:, pl.ds(pl.multiple_of(s * rows, 8), rows), :], sems.at[at]
        )

    @pl.when(step == 0)
    def _():
        norms[...] = jnp.zeros_like(norms)

    @pl.when(step >= 2)
    def _():
        copy(step - 2, slot).wait()

    for p in range(PAIR):
        cg, ng = coded(tg[p] + og[p].astype(jnp.float32))
        cu, nu = coded(tu[p] + ou[p].astype(jnp.float32))
        both = jnp.concatenate([cg, cu], axis=0)
        turned = both.T.astype(jnp.bfloat16).reshape(parts, width, both.shape[0])
        codes[slot, :, p * width : (p + 1) * width, :] = turned
        at = (step * PAIR + p) * 2
        norms[pl.ds(at, 1), :] = ng
        norms[pl.ds(at + 1, 1), :] = nu
    copy(step, slot).start()

    @pl.when(step == steps - 1)
    def _():
        turned = norms[...].T.reshape(parts, width // 8, 8, 128)
        packed = turned[:, 0]
        for k in range(1, width // 8):
            packed = packed + pltpu.roll(turned[:, k], 32 * k, 2)
        norm_rows[...] = packed.astype(jnp.bfloat16)
        last = pltpu.make_async_copy(
            norm_rows, out.at[:, pl.ds(steps * rows, 8), :], norm_sem
        )
        last.start()
        copy(step - 1, 1 - slot).wait()
        copy(step, slot).wait()
        last.wait()


def encode(parts, tg, og, tu, ou):
    experts, mine, columns = tg.shape
    width = columns // parts
    block = lambda: pl.BlockSpec((PAIR, mine, columns), lambda s: (s, 0, 0))
    return pl.pallas_call(
        functools.partial(encode_kernel, parts),
        grid=(experts // PAIR,),
        in_specs=[block() for _ in range(4)],
        out_specs=pl.BlockSpec(memory_space=pl.ANY),
        out_shape=jax.ShapeDtypeStruct((parts, experts * width + 8, 2 * mine), jnp.bfloat16),
        scratch_shapes=[
            pltpu.VMEM((2, parts, PAIR * width, 2 * mine), jnp.bfloat16),
            pltpu.VMEM((128, columns), jnp.float32),
            pltpu.VMEM((parts, 8, 2 * mine), jnp.bfloat16),
            pltpu.SemaphoreType.DMA((2,)),
            pltpu.SemaphoreType.DMA,
        ],
        name="encode",
    )(tg, og, tu, ou)


def decode_kernel(code, norm, ready_g, ready_u, scale_g, scale_u, sums):
    step = pl.program_id(0)
    parts = code.shape[0]
    width = code.shape[1] // PAIR
    tiles = width // 8
    total = parts * code.shape[2] // 2
    lane = lax.broadcasted_iota(jnp.int32, (8, 128), 1)
    left = lane < 64

    @pl.when(step == 0)
    def _():
        sums[...] = jnp.zeros_like(sums)

    source = lax.broadcasted_iota(jnp.int32, (128, PAIR * tiles * 128), 0)
    goal = lax.broadcasted_iota(jnp.int32, (128, PAIR * tiles * 128), 1)
    tile, at = goal // 128, goal % 128
    wanted = 32 * (tile % tiles) + 2 * (step * PAIR + tile // tiles) + at // 64
    pick = (source == wanted).astype(jnp.bfloat16)
    spread = jnp.dot(norm[...].reshape(parts * 8, 128), pick, preferred_element_type=jnp.float32)
    spread = spread.reshape(parts, 8, PAIR * tiles * 128)

    c = code[...].astype(jnp.float32)
    for p in range(PAIR):
        outs_g, outs_u = [], []
        for k in range(tiles):
            at = p * tiles + k
            tile = c[:, at * 8 : (at + 1) * 8, :]
            size = jnp.exp2(jnp.log2(jnp.abs(tile)) * (1.0 / POWER))
            size = size * spread[:, :, at * 128 : (at + 1) * 128]
            acc = jnp.sum(size, axis=0)
            sg = jnp.sum(jnp.where(left, acc, 0.0), axis=1, keepdims=True) * (1.0 / total)
            su = jnp.sum(jnp.where(left, 0.0, acc), axis=1, keepdims=True) * (1.0 / total)
            chosen = 2 * (step * PAIR + p)
            sums[k * 8 : (k + 1) * 8, :] += jnp.where(
                lane == chosen, sg, jnp.where(lane == chosen + 1, su, 0.0)
            )
            size = size * jnp.where(left, 1.0 / sg, 1.0 / su)[None]
            y = jnp.where(tile < 0, -size, size).reshape(parts // 2, 2, 8, 128)
            turned = pltpu.roll(y.reshape(parts, 8, 128), 64, 2).reshape(parts // 2, 2, 8, 128)
            outs_g.append(jnp.where(left, y[:, 0], turned[:, 1]))
            outs_u.append(jnp.where(left, turned[:, 0], y[:, 1]))
        g = jnp.concatenate(outs_g, axis=1).astype(jnp.bfloat16)
        u = jnp.concatenate(outs_u, axis=1).astype(jnp.bfloat16)
        for t in range(parts // 2):
            ready_g[p, :, t * 128 : (t + 1) * 128] = g[t]
            ready_u[p, :, t * 128 : (t + 1) * 128] = u[t]

    @pl.when(step == pl.num_programs(0) - 1)
    def _():
        turned = jnp.concatenate(
            [sums[...], jnp.zeros((128 - width, 128), jnp.float32)], axis=0
        ).T
        turned = turned[:32].reshape(16, 2, 128)
        scale_g[...] = turned[:, 0, :width]
        scale_u[...] = turned[:, 1, :width]


def decode(experts, arrived):
    parts, rows, lanes = arrived.shape
    width = (rows - 8) // experts
    total = parts * lanes // 2
    ready = jax.ShapeDtypeStruct((experts, width, total), jnp.bfloat16)
    scale = jax.ShapeDtypeStruct((experts, width), jnp.float32)
    out = lambda: pl.BlockSpec((PAIR, width, total), lambda s: (s, 0, 0))
    small = lambda: pl.BlockSpec((experts, width), lambda s: (0, 0))
    return pl.pallas_call(
        decode_kernel,
        grid=(experts // PAIR,),
        in_specs=[
            pl.BlockSpec((parts, PAIR * width, lanes), lambda s: (0, s, 0)),
            pl.BlockSpec((parts, 8, lanes), lambda s: (0, experts * width // 8, 0)),
        ],
        out_specs=[out(), out(), small(), small()],
        out_shape=[ready, ready, scale, scale],
        scratch_shapes=[pltpu.VMEM((width, 128), jnp.float32)],
        name="decode",
    )(arrived, arrived)


def swapped(block, axis, bit):
    n = lax.axis_size(axis)
    other = lax.ppermute(block, axis, [(i, i ^ bit) for i in range(n)])
    high = (lax.axis_index(axis) & bit) != 0
    return jnp.where(high, other, block), jnp.where(high, block, other)


def gathered(block, axis):
    shape = block.shape
    bit = lax.axis_size(axis) // 2
    held = 1
    while bit:
        low, high = swapped(block, axis, bit)
        low, high = (a.reshape(held, -1, *shape[1:]) for a in (low, high))
        block = jnp.stack([low, high], axis=1).reshape(-1, *shape[1:])
        held *= 2
        bit //= 2
    return block


def per_device(train_gate, other_gate, train_up, other_up, router_weight, router_gain):
    experts, mine, columns = train_gate.shape
    parts = lax.axis_size("fsdp")
    codes = encode(parts, train_gate, other_gate, train_up, other_up)
    arrived = lax.all_to_all(codes, "fsdp", split_axis=0, concat_axis=0, tiled=True)

    rows, wide = router_weight.shape
    part = (router_weight * router_gain[:, None]).astype(jnp.bfloat16).T
    part = part.reshape(1, 8, -1)
    part, _ = lax.optimization_barrier((part, codes))
    group = gathered(part, "fsdp").reshape(parts, wide, rows)
    group = group.transpose(1, 0, 2).reshape(wide, parts * rows)
    serve_router = gathered(group, "ep").T

    ready_gate, ready_up, scale_gate, scale_up = decode(experts, arrived)
    return (
        jnp.swapaxes(ready_gate, 1, 2),
        jnp.swapaxes(ready_up, 1, 2),
        scale_gate,
        scale_up,
        serve_router,
    )


def solution(mesh):
    in_specs = (
        P("ep", "fsdp", None),
        P("ep", "fsdp", None),
        P("ep", "fsdp", None),
        P("ep", "fsdp", None),
        P("fsdp", "ep"),
        P("fsdp"),
    )
    out_specs = (
        P("ep", None, "fsdp"),
        P("ep", None, "fsdp"),
        P("ep", "fsdp"),
        P("ep", "fsdp"),
        P(),
    )
    return jax.shard_map(
        per_device, mesh=mesh, in_specs=in_specs, out_specs=out_specs, check_vma=False
    )
```

time: 188 us -> 142 us (0.76)
  local copies, waits for them, and re-layouts: 51 us -> 4.97 us
  Pallas kernels: 0 us -> 17.7 us
  starting transfers between devices: 34.1 us -> 27.2 us
  other arithmetic: 7.89 us -> 1.22 us
  waiting for transfers between devices: 90.7 us -> 87.7 us
    all_to_all x5 -> x1, waiting for transfers between devices: 90.7 us -> 0.01 us  [per_device(): lax.all_to_all(codes, 'fsdp', split_axis=0, concat_axis=0, tiled=True)]
    ppermute x0 -> x8, waiting for transfers between devices: none -> 87.7 us  [swapped(): other = lax.ppermute(block, axis, [(i, i ^ bit) for i in range(n)])]
    all_to_all x5 -> x1, starting transfers between devices: 34.1 us -> 11.6 us  [per_device(): lax.all_to_all(codes, 'fsdp', split_axis=0, concat_axis=0, tiled=True)]
    pallas_call x0 -> x2, Pallas kernels: none -> 17.7 us  [the longest x1 9.08 us: encode(): pl.pallas_call(functools.partial(encode_kernel, parts), grid=(experts //...]
    unnamed x20 -> x7, local copies, waits for them, and re-layouts: 19.6 us -> 3.7 us
    ppermute x0 -> x8, starting transfers between devices: none -> 15.6 us  [swapped(): other = lax.ppermute(block, axis, [(i, i ^ bit) for i in range(n)])]
    slice x5 -> x0, local copies, waits for them, and re-layouts: 12.9 us -> none  [in_one_piece(): outs.append(lax.slice_in_dim(filled, at, at + a.shape[along], axis=along))]
    concatenate x1 -> x0, local copies, waits for them, and re-layouts: 9.47 us -> none  [in_one_piece(): both = jnp.concatenate(arrays, axis=along)]
  transfers between devices with their start and end apart: 5 -> 9, of which waited for: 4 -> 8; matrix products, arithmetic and copies ran while one was open for 14% -> 3% of each run, Pallas kernels for 0% -> 0%
where the time goes in v1:
time: 142 us; the launch traced here: 140 us
  waiting for transfers between devices  87.7 us (62%)
  starting transfers between devices  27.2 us (19%)
  Pallas kernels  17.7 us (12%)
  local copies, waits for them, and re-layouts  4.97 us (4%)
    ppermute x8, waiting for transfers between devices, swapped(): other = lax.ppermute(block, axis, [(i, i ^ bit) for i in range(n)])  87.7 us
    ppermute x8, starting transfers between devices, swapped(): other = lax.ppermute(block, axis, [(i, i ^ bit) for i in range(n)])  15.6 us
    all_to_all x1, starting transfers between devices, per_device(): lax.all_to_all(codes, 'fsdp', split_axis=0, concat_axis=0, tiled=True)  11.6 us
    pallas_call x1, Pallas kernels, encode(): pl.pallas_call(functools.partial(encode_kernel, parts), grid=(experts //...  9.08 us
    pallas_call x1, Pallas kernels, decode(): pl.pallas_call(decode_kernel, grid=(experts // PAIR,), in_specs=[pl.Block...  8.59 us
    unnamed x7, local copies, waits for them, and re-layouts  3.7 us
  transfers between devices with their start and end apart: 9, of which 8 were waited for; matrix products, arithmetic and copies ran while one was open for 3% of the time, Pallas kernels for 0%

profile of v1, /device:TPU:22, one launch (start us, length us, event | category | flops | bytes accessed | tf_op | source)
XLA Modules:
  0.0 139.6 jit_solution(14061679663119982410)
XLA Ops:
  0.6 9.1 %encode.1 = bf16[32,392,128]{2,1,0:T(8,128)(2,1)} custom-call(f32[16,64,768]{2,1,0:T(8,128)} %tg.1, bf16[16,64,768]{2,1,0:T(8,128)(2,1)} %og.1, f32[16,64,768]{2,1,0:T(8,128)} %tu.1, bf16[16,64,768]{2,1,0:T(8,128)(2,1)} %ou.1), custom_call_target="tpu_custom_call" | custom-call | tf_op jit(solution)/shard_map/encode/pallas_call | solution.py:77
  9.7 0.0 copy-start.1
  9.7 0.0 copy-start.2
  9.7 11.6 %all-to-all-start = ((bf16[32,392,128]{2,1,0:T(8,128)(2,1)}), bf16[32,392,128]{2,1,0:T(8,128)(2,1)S(1)}, u32[]{:S(2)}, u32[]{:S(2)}) async-start(bf16[32,392,128]{2,1,0:T(8,128)(2,1)} %encode.1), calls=%async_computation | async-start | bytes 6422528 | tf_op jit(solution)/shard_map/all_to_all | solution.py:197
  21.4 0.0 copy-done.1
  21.4 0.0 copy-done.2
  21.4 0.1 reshape.38
  21.5 5.4 %collective-permute-start = (bf16[1,8,128]{2,1,0:T(8,128)(2,1)S(1)}, bf16[1,8,128]{2,1,0:T(8,128)(2,1)S(1)}, u32[]{:S(2)}, u32[]{:S(2)}) collective-permute-start(bf16[1,8,128]{2,1,0:T(8,128)(2,1)S(1)} %reshape.38), channel_id=1, source_target_pairs={{0,16},{1,17},{2,18},{3,19},{4,20},{5,21},{6,22},{7,23},{8,24},{9,... | collective-permute-start | bytes 6152 | tf_op jit(solution)/shard_map/ppermute | solution.py:175
  26.9 66.9 %collective-permute-done = bf16[1,8,128]{2,1,0:T(8,128)(2,1)S(1)} collective-permute-done((bf16[1,8,128]{2,1,0:T(8,128)(2,1)S(1)}, bf16[1,8,128]{2,1,0:T(8,128)(2,1)S(1)}, u32[]{:S(2)}, u32[]{:S(2)}) %collective-permute-start) | collective-permute-done | bytes 2080 | tf_op jit(solution)/shard_map/ppermute | solution.py:175
  93.8 2.8 %collective-permute-start.1 = (bf16[2,8,128]{2,1,0:T(8,128)(2,1)S(1)}, bf16[2,8,128]{2,1,0:T(8,128)(2,1)S(1)}, u32[]{:S(2)}, u32[]{:S(2)}) collective-permute-start(bf16[2,8,128]{2,1,0:T(8,128)(2,1)S(1)} %maximum_bitcast_fusion), channel_id=1, source_target_pairs={{0,8},{1,9},{2,10},{3,11},{4,12},{5,13},{6,14},{7,15},{8,0},{9,1},... | collective-permute-start | bytes 12296 | tf_op jit(solution)/shard_map/ppermute | solution.py:175
  96.6 1.8 %collective-permute-done.1 = bf16[2,8,128]{2,1,0:T(8,128)(2,1)S(1)} collective-permute-done((bf16[2,8,128]{2,1,0:T(8,128)(2,1)S(1)}, bf16[2,8,128]{2,1,0:T(8,128)(2,1)S(1)}, u32[]{:S(2)}, u32[]{:S(2)}) %collective-permute-start.1) | collective-permute-done | bytes 4128 | tf_op jit(solution)/shard_map/ppermute | solution.py:175
  98.4 2.8 %collective-permute-start.2 = (bf16[4,8,128]{2,1,0:T(8,128)(2,1)S(1)}, bf16[4,8,128]{2,1,0:T(8,128)(2,1)S(1)}, u32[]{:S(2)}, u32[]{:S(2)}) collective-permute-start(bf16[4,8,128]{2,1,0:T(8,128)(2,1)S(1)} %bitcast.75), channel_id=1, source_target_pairs={{0,4},{1,5},{2,6},{3,7},{4,0},{5,1},{6,2},{7,3},{8,12},{9,13},{10,... | collective-permute-start | bytes 24584 | tf_op jit(solution)/shard_map/ppermute | solution.py:175
  101.2 1.6 %collective-permute-done.2 = bf16[4,8,128]{2,1,0:T(8,128)(2,1)S(1)} collective-permute-done((bf16[4,8,128]{2,1,0:T(8,128)(2,1)S(1)}, bf16[4,8,128]{2,1,0:T(8,128)(2,1)S(1)}, u32[]{:S(2)}, u32[]{:S(2)}) %collective-permute-start.2) | collective-permute-done | bytes 8224 | tf_op jit(solution)/shard_map/ppermute | solution.py:175
  102.9 0.9 collective-permute-start.3
  103.8 4.4 %collective-permute-done.3 = bf16[8,8,128]{2,1,0:T(8,128)(2,1)S(1)} collective-permute-done((bf16[8,8,128]{2,1,0:T(8,128)(2,1)S(1)}, bf16[8,8,128]{2,1,0:T(8,128)(2,1)S(1)}, u32[]{:S(2)}, u32[]{:S(2)}) %collective-permute-start.3) | collective-permute-done | bytes 16416 | tf_op jit(solution)/shard_map/ppermute | solution.py:175
  108.2 1.2 collective-permute-start.4
  109.4 2.8 %collective-permute-done.4 = bf16[16,8,128]{2,1,0:T(8,128)(2,1)S(1)} collective-permute-done((bf16[16,8,128]{2,1,0:T(8,128)(2,1)S(1)}, bf16[16,8,128]{2,1,0:T(8,128)(2,1)S(1)}, u32[]{:S(2)}, u32[]{:S(2)}) %collective-permute-start.4) | collective-permute-done | bytes 32800 | tf_op jit(solution)/shard_map/ppermute | solution.py:175
  112.3 0.1 reshape_reshape.3
  112.4 0.2 reshape.43
  112.6 1.5 %collective-permute-start.5 = (bf16[16,2048]{1,0:T(8,128)(2,1)S(1)}, bf16[16,2048]{1,0:T(8,128)(2,1)S(1)}, u32[]{:S(2)}, u32[]{:S(2)}) collective-permute-start(bf16[16,2048]{1,0:T(8,128)(2,1)S(1)} %reshape.43), channel_id=1, source_target_pairs={{0,128},{32,160},{64,192},{96,224},{128,0},{160,32},{192,64},{224,... | collective-permute-start | bytes 196616 | tf_op jit(solution)/shard_map/ppermute | solution.py:175
  114.1 4.4 %collective-permute-done.5 = bf16[16,2048]{1,0:T(8,128)(2,1)S(1)} collective-permute-done((bf16[16,2048]{1,0:T(8,128)(2,1)S(1)}, bf16[16,2048]{1,0:T(8,128)(2,1)S(1)}, u32[]{:S(2)}, u32[]{:S(2)}) %collective-permute-start.5) | collective-permute-done | bytes 65568 | tf_op jit(solution)/shard_map/ppermute | solution.py:175
  118.5 0.9 collective-permute-start.6
  119.4 4.1 %collective-permute-done.6 = bf16[32,2048]{1,0:T(8,128)(2,1)S(1)} collective-permute-done((bf16[32,2048]{1,0:T(8,128)(2,1)S(1)}, bf16[32,2048]{1,0:T(8,128)(2,1)S(1)}, u32[]{:S(2)}, u32[]{:S(2)}) %collective-permute-start.6) | collective-permute-done | bytes 131104 | tf_op jit(solution)/shard_map/ppermute | solution.py:175
  123.7 0.1 collective-permute-start.7
  123.8 1.6 %collective-permute-done.7 = bf16[64,2048]{1,0:T(8,128)(2,1)} collective-permute-done((bf16[64,2048]{1,0:T(8,128)(2,1)S(1)}, bf16[64,2048]{1,0:T(8,128)(2,1)}, u32[]{:S(2)}, u32[]{:S(2)}) %collective-permute-start.7) | collective-permute-done | bytes 262176 | tf_op jit(solution)/shard_map/ppermute | solution.py:175
  125.4 1.0 broadcast_select_fusion.1
  126.4 0.1 pad_maximum_fusion
  126.5 0.8 copy.36
  127.3 2.0 %copy.37 = bf16[2048,128]{1,0:T(8,128)(2,1)} copy(bf16[2048,128]{0,1:T(8,128)(2,1)} %bitcast.65) | data formatting | bytes 1048576
  129.3 0.0 all-to-all-done.code.norm
  129.3 0.0 copy-start
  129.3 1.6 %copy-done = bf16[32,392,128]{2,1,0:T(8,128)(2,1)} copy-done((bf16[32,392,128]{2,1,0:T(8,128)(2,1)}, bf16[32,392,128]{2,1,0:T(8,128)(2,1)S(1)}, u32[]{:S(2)}) %copy-start) | copy-done | bytes 3211288
  131.0 8.6 %decode.1 = (bf16[16,24,2048]{2,1,0:T(8,128)(2,1)}, bf16[16,24,2048]{2,1,0:T(8,128)(2,1)}, f32[16,24]{1,0:T(8,128)}, f32[16,24]{1,0:T(8,128)}) custom-call(bf16[32,392,128]{2,1,0:T(8,128)(2,1)} %copy-done, bf16[32,392,128]{2,1,0:T(8,128)(2,1)} %copy-done), custom_call_target="tpu_custom_call" | custom-call | tf_op jit(solution)/shard_map/decode/pallas_call | solution.py:159
  (20 shorter events, 0.3 us)
Async XLA Ops:
  9.7 11.6 %copy-start.1 = (f32[64,16]{0,1:T(8,128)S(1)}, f32[64,16]{0,1:T(8,128)}, u32[]{:S(2)}) copy-start(f32[64,16]{0,1:T(8,128)} %param.10) | copy-start | bytes 12292
  9.7 11.6 %copy-start.2 = (f32[64]{0:T(128)S(1)}, f32[64]{0:T(128)}, u32[]{:S(2)}) copy-start(f32[64]{0:T(128)} %param.11) | copy-start | bytes 772
  9.7 119.6 %all-to-all-start = ((bf16[32,392,128]{2,1,0:T(8,128)(2,1)}), bf16[32,392,128]{2,1,0:T(8,128)(2,1)S(1)}, u32[]{:S(2)}, u32[]{:S(2)}) async-start(bf16[32,392,128]{2,1,0:T(8,128)(2,1)} %encode.1), calls=%async_computation | async-start | bytes 6422528 | tf_op jit(solution)/shard_map/all_to_all | solution.py:197
  21.5 72.3 %collective-permute-start = (bf16[1,8,128]{2,1,0:T(8,128)(2,1)S(1)}, bf16[1,8,128]{2,1,0:T(8,128)(2,1)S(1)}, u32[]{:S(2)}, u32[]{:S(2)}) collective-permute-start(bf16[1,8,128]{2,1,0:T(8,128)(2,1)S(1)} %reshape.38), channel_id=1, source_target_pairs={{0,16},{1,17},{2,18},{3,19},{4,20},{5,21},{6,22},{7,23},{8,24},{9,... | collective-permute-start | bytes 6152 | tf_op jit(solution)/shard_map/ppermute | solution.py:175
  93.8 4.6 %collective-permute-start.1 = (bf16[2,8,128]{2,1,0:T(8,128)(2,1)S(1)}, bf16[2,8,128]{2,1,0:T(8,128)(2,1)S(1)}, u32[]{:S(2)}, u32[]{:S(2)}) collective-permute-start(bf16[2,8,128]{2,1,0:T(8,128)(2,1)S(1)} %maximum_bitcast_fusion), channel_id=1, source_target_pairs={{0,8},{1,9},{2,10},{3,11},{4,12},{5,13},{6,14},{7,15},{8,0},{9,1},... | collective-permute-start | bytes 12296 | tf_op jit(solution)/shard_map/ppermute | solution.py:175
  98.4 4.4 %collective-permute-start.2 = (bf16[4,8,128]{2,1,0:T(8,128)(2,1)S(1)}, bf16[4,8,128]{2,1,0:T(8,128)(2,1)S(1)}, u32[]{:S(2)}, u32[]{:S(2)}) collective-permute-start(bf16[4,8,128]{2,1,0:T(8,128)(2,1)S(1)} %bitcast.75), channel_id=1, source_target_pairs={{0,4},{1,5},{2,6},{3,7},{4,0},{5,1},{6,2},{7,3},{8,12},{9,13},{10,... | collective-permute-start | bytes 24584 | tf_op jit(solution)/shard_map/ppermute | solution.py:175
  102.9 5.3 %collective-permute-start.3 = (bf16[8,8,128]{2,1,0:T(8,128)(2,1)S(1)}, bf16[8,8,128]{2,1,0:T(8,128)(2,1)S(1)}, u32[]{:S(2)}, u32[]{:S(2)}) collective-permute-start(bf16[8,8,128]{2,1,0:T(8,128)(2,1)S(1)} %bitcast.74), channel_id=1, source_target_pairs={{0,2},{1,3},{2,0},{3,1},{4,6},{5,7},{6,4},{7,5},{8,10},{9,11},{10,... | collective-permute-start | bytes 49160 | tf_op jit(solution)/shard_map/ppermute | solution.py:175
  108.2 4.0 %collective-permute-start.4 = (bf16[16,8,128]{2,1,0:T(8,128)(2,1)S(1)}, bf16[16,8,128]{2,1,0:T(8,128)(2,1)S(1)}, u32[]{:S(2)}, u32[]{:S(2)}) collective-permute-start(bf16[16,8,128]{2,1,0:T(8,128)(2,1)S(1)} %bitcast.73), channel_id=1, source_target_pairs={{0,1},{1,0},{2,3},{3,2},{4,5},{5,4},{6,7},{7,6},{8,9},{9,8},{10,11... | collective-permute-start | bytes 98312 | tf_op jit(solution)/shard_map/ppermute | solution.py:175
  112.6 5.9 %collective-permute-start.5 = (bf16[16,2048]{1,0:T(8,128)(2,1)S(1)}, bf16[16,2048]{1,0:T(8,128)(2,1)S(1)}, u32[]{:S(2)}, u32[]{:S(2)}) collective-permute-start(bf16[16,2048]{1,0:T(8,128)(2,1)S(1)} %reshape.43), channel_id=1, source_target_pairs={{0,128},{32,160},{64,192},{96,224},{128,0},{160,32},{192,64},{224,... | collective-permute-start | bytes 196616 | tf_op jit(solution)/shard_map/ppermute | solution.py:175
  118.5 5.1 %collective-permute-start.6 = (bf16[32,2048]{1,0:T(8,128)(2,1)S(1)}, bf16[32,2048]{1,0:T(8,128)(2,1)S(1)}, u32[]{:S(2)}, u32[]{:S(2)}) collective-permute-start(bf16[32,2048]{1,0:T(8,128)(2,1)S(1)} %bitcast.69), channel_id=1, source_target_pairs={{0,64},{32,96},{64,0},{96,32},{128,192},{160,224},{192,128},{224,1... | collective-permute-start | bytes 393224 | tf_op jit(solution)/shard_map/ppermute | solution.py:175
  123.7 1.8 %collective-permute-start.7 = (bf16[64,2048]{1,0:T(8,128)(2,1)S(1)}, bf16[64,2048]{1,0:T(8,128)(2,1)}, u32[]{:S(2)}, u32[]{:S(2)}) collective-permute-start(bf16[64,2048]{1,0:T(8,128)(2,1)S(1)} %bitcast.66), channel_id=1, source_target_pairs={{0,32},{32,0},{64,96},{96,64},{128,160},{160,128},{192,224},{224,1... | collective-permute-start | bytes 786440 | tf_op jit(solution)/shard_map/ppermute | solution.py:175
  129.3 1.7 %copy-start = (bf16[32,392,128]{2,1,0:T(8,128)(2,1)}, bf16[32,392,128]{2,1,0:T(8,128)(2,1)S(1)}, u32[]{:S(2)}) copy-start(bf16[32,392,128]{2,1,0:T(8,128)(2,1)S(1)} %all-to-all-done.code.norm) | copy-start | bytes 9633796

commit v2 on v1

v2 whole, which is shorter than its diff:
```python
import functools

import jax
import jax.numpy as jnp
from jax import lax
from jax.experimental import pallas as pl
from jax.experimental.pallas import tpu as pltpu
from jax.sharding import PartitionSpec as P

POWER = 15
SPREAD = 5.0
LEAST = 1e-30
SMALLEST = 2.0**-126
PAIR = 2
LANES = 128
MIB = 2**20


def coded(latest):
    mean = jnp.sum(jnp.abs(latest), axis=0, keepdims=True) * (1.0 / (latest.shape[0] * SPREAD))
    norm = jnp.maximum(mean, LEAST).astype(jnp.bfloat16).astype(jnp.float32)
    v = latest * (1.0 / norm)
    v2 = v * v
    v4 = v2 * v2
    v8 = v4 * v4
    return (v8 * v4) * (v2 * v), norm


def coded_pair(parts, tg, og, tu, ou, p):
    cg, ng = coded(tg[p] + og[p].astype(jnp.float32))
    cu, nu = coded(tu[p] + ou[p].astype(jnp.float32))
    turned = jnp.concatenate([cg, cu], axis=0).T.reshape(parts, -1, LANES)
    return turned, ng, nu


def first_kernel(parts, tg, og, tu, ou, weight, gain, out, norms):
    width = tg.shape[2] // parts
    rows = PAIR * width
    norms[...] = jnp.zeros_like(norms)
    for p in range(PAIR):
        codes, ng, nu = coded_pair(parts, tg, og, tu, ou, p)
        for k in range(0, width, 8):
            out[:, p * width + k : p * width + k + 8, :] = codes[:, k : k + 8].astype(jnp.bfloat16)
        norms[2 * p : 2 * p + 1, :] = ng
        norms[2 * p + 1 : 2 * p + 2, :] = nu
    part = weight[...] * gain[...]
    part = jnp.concatenate([part[:8], part[8:]], axis=1).astype(jnp.bfloat16)
    out[:, rows:, :] = jnp.broadcast_to(part[None], (parts, 8, LANES))


def encode_first(parts, tg, og, tu, ou, weight, gain):
    _, mine, columns = tg.shape
    width = columns // parts
    block = lambda: pl.BlockSpec((PAIR, mine, columns), lambda s: (0, 0, 0))
    whole = lambda a: pl.BlockSpec(a.shape, lambda s: (0,) * len(a.shape))
    out = jax.ShapeDtypeStruct((parts, PAIR * width + 8, LANES), jnp.bfloat16)
    norms = jax.ShapeDtypeStruct((8, columns), jnp.float32)
    return pl.pallas_call(
        functools.partial(first_kernel, parts),
        grid=(1,),
        in_specs=[block() for _ in range(4)] + [whole(weight), whole(gain)],
        out_specs=[whole(out), whole(norms)],
        out_shape=[out, norms],
        cost_estimate=pl.CostEstimate(flops=50_000_000, bytes_accessed=1_700_000, transcendentals=0),
        name="encode_first",
    )(tg, og, tu, ou, weight, gain)


def rest_kernel(parts, tg, og, tu, ou, before, out, codes, norms, norm_rows, sems, norm_sem):
    step = pl.program_id(0)
    steps = pl.num_programs(0)
    width = tg.shape[2] // parts
    rows = PAIR * width
    slot = lax.rem(step, 2)

    def copy(s, at):
        return pltpu.make_async_copy(
            codes.at[at], out.at[:, pl.ds(pl.multiple_of(s * rows, 8), rows), :], sems.at[at]
        )

    @pl.when(step == 0)
    def _():
        norms[...] = jnp.zeros_like(norms)
        norms[0:8, :] = before[...]

    @pl.when(step >= 2)
    def _():
        copy(step - 2, slot).wait()

    for p in range(PAIR):
        turned, ng, nu = coded_pair(parts, tg, og, tu, ou, p)
        for k in range(0, width, 8):
            codes[slot, :, p * width + k : p * width + k + 8, :] = turned[:, k : k + 8].astype(
                jnp.bfloat16
            )
        at = ((step + 1) * PAIR + p) * 2
        norms[pl.ds(at, 1), :] = ng
        norms[pl.ds(at + 1, 1), :] = nu
    copy(step, slot).start()

    @pl.when(step == steps - 1)
    def _():
        turned = norms[...].T.reshape(parts, width // 8, 8, LANES)
        packed = turned[:, 0]
        for k in range(1, width // 8):
            packed = packed + pltpu.roll(turned[:, k], 32 * k, 2)
        norm_rows[...] = packed.astype(jnp.bfloat16)
        last = pltpu.make_async_copy(
            norm_rows, out.at[:, pl.ds(steps * rows, 8), :], norm_sem
        )
        last.start()
        copy(step - 1, 1 - slot).wait()
        copy(step, slot).wait()
        last.wait()


def encode_rest(parts, tg, og, tu, ou, before):
    experts, mine, columns = tg.shape
    width = columns // parts
    steps = experts // PAIR - 1
    block = lambda: pl.BlockSpec((PAIR, mine, columns), lambda s: (s + 1, 0, 0))
    return pl.pallas_call(
        functools.partial(rest_kernel, parts),
        grid=(steps,),
        in_specs=[block() for _ in range(4)] + [pl.BlockSpec(before.shape, lambda s: (0, 0))],
        out_specs=pl.BlockSpec(memory_space=pl.ANY),
        out_shape=jax.ShapeDtypeStruct((parts, steps * PAIR * width + 8, LANES), jnp.bfloat16),
        scratch_shapes=[
            pltpu.VMEM((2, parts, PAIR * width, LANES), jnp.bfloat16),
            pltpu.VMEM((LANES, columns), jnp.float32),
            pltpu.VMEM((parts, 8, LANES), jnp.bfloat16),
            pltpu.SemaphoreType.DMA((2,)),
            pltpu.SemaphoreType.DMA,
        ],
        cost_estimate=pl.CostEstimate(flops=400_000_000, bytes_accessed=11_000_000, transcendentals=0),
        name="encode_rest",
    )(tg, og, tu, ou, before)


def decode_kernel(first, rest, out_g, out_u, scale_g, scale_u, pick, spread, values, sums, ready, sems):
    parts = first.shape[0]
    rows = first.shape[1] - 8
    width = rows // PAIR
    tiles = width // 8
    steps = rest.shape[1] // rows + 1
    total = parts * LANES // 2
    half = LANES // 2
    lane = lax.broadcasted_iota(jnp.int32, (rows, LANES), 1)
    left = lane < half
    sums[...] = jnp.zeros_like(sums)

    source = lax.broadcasted_iota(jnp.int32, pick.shape, 0)
    goal = lax.broadcasted_iota(jnp.int32, pick.shape, 1)
    tile, at = goal // LANES, goal % LANES
    wanted = 32 * (tile % tiles) + 2 * (tile // tiles) + at // half
    pick[...] = (source == wanted).astype(jnp.bfloat16)

    def copies(step, slot):
        where = pl.ds(pl.multiple_of(step * rows, rows), rows)
        return [
            pltpu.make_async_copy(ready.at[slot, m], out.at[where, :], sems.at[slot, m])
            for m, out in enumerate((out_g, out_u))
        ]

    def one(step, code, start):
        slot = lax.rem(step, 2)
        norm = rest[:, (steps - 1) * rows :, :].reshape(parts * 8, LANES).astype(jnp.float32)
        norm = pltpu.roll(norm, lax.rem(LANES - 2 * PAIR * step, LANES), 1)
        spread[...] = jnp.dot(
            norm.astype(jnp.bfloat16), pick[...], preferred_element_type=jnp.float32
        )
        acc = jnp.zeros((rows, LANES), jnp.float32)
        for src in range(parts):
            c = code[src, pl.ds(start, rows), :].astype(jnp.float32)
            scale = jnp.concatenate(
                [
                    spread[src * 8 : src * 8 + 8, k * LANES : (k + 1) * LANES]
                    for k in range(PAIR * tiles)
                ],
                axis=0,
            )
            size = jnp.log2(jnp.maximum(jnp.abs(c), SMALLEST))
            value = (c * scale) * jnp.exp2(size * (1.0 / POWER - 1.0))
            acc = acc + jnp.abs(value)
            values[src] = value
        sg = jnp.sum(jnp.where(left, acc, 0.0), axis=1, keepdims=True) * (1.0 / total)
        su = jnp.sum(jnp.where(left, 0.0, acc), axis=1, keepdims=True) * (1.0 / total)
        sums[...] += jnp.where(
            lane == 2 * step, sg, jnp.where(lane == 2 * step + 1, su, 0.0)
        )
        factor = jnp.where(left, 1.0 / sg, 1.0 / su)

        @pl.when(step >= 2)
        def _():
            for copy in copies(step - 2, slot):
                copy.wait()

        for t in range(parts // 2):
            even, odd = values[2 * t] * factor, values[2 * t + 1] * factor
            g = jnp.where(left, even, pltpu.roll(odd, half, 1))
            u = jnp.where(left, pltpu.roll(even, half, 1), odd)
            for m, whole in enumerate((g, u)):
                for k in range(0, rows, 8):
                    ready[slot, m, k : k + 8, t * LANES : (t + 1) * LANES] = whole[
                        k : k + 8
                    ].astype(jnp.bfloat16)
        for copy in copies(step, slot):
            copy.start()

    one(jnp.int32(0), first, 0)

    @pl.loop(1, steps)
    def _(step):
        one(step, rest, pl.multiple_of((step - 1) * rows, 8))

    turned = jnp.concatenate(
        [sums[...], jnp.zeros((LANES - rows, LANES), jnp.float32)], axis=0
    ).T
    turned = turned[: 2 * steps].reshape(steps, 2, LANES)
    for p in range(PAIR):
        scale_g[pl.ds(p, steps, stride=PAIR), :] = turned[:, 0, p * width : (p + 1) * width]
        scale_u[pl.ds(p, steps, stride=PAIR), :] = turned[:, 1, p * width : (p + 1) * width]
    for step in (steps - 2, steps - 1):
        for copy in copies(step, step % 2):
            copy.wait()


def decode(experts, first, rest):
    parts, rows, lanes = first.shape
    rows = rows - 8
    width = rows // PAIR
    total = parts * lanes // 2
    ready = jax.ShapeDtypeStruct((experts * width, total), jnp.bfloat16)
    scale = jax.ShapeDtypeStruct((experts, width), jnp.float32)
    vmem, anywhere = pl.BlockSpec(memory_space=pltpu.VMEM), pl.BlockSpec(memory_space=pl.ANY)
    ready_g, ready_u, scale_g, scale_u = pl.pallas_call(
        decode_kernel,
        in_specs=[vmem, vmem],
        out_specs=[anywhere, anywhere, vmem, vmem],
        out_shape=[ready, ready, scale, scale],
        scratch_shapes=[
            pltpu.VMEM((lanes, rows // 8 * lanes), jnp.bfloat16),
            pltpu.VMEM((parts * 8, rows // 8 * lanes), jnp.float32),
            pltpu.VMEM((parts, rows, lanes), jnp.float32),
            pltpu.VMEM((rows, lanes), jnp.float32),
            pltpu.VMEM((2, 2, rows, total), jnp.bfloat16),
            pltpu.SemaphoreType.DMA((2, 2)),
        ],
        compiler_params=pltpu.CompilerParams(vmem_limit_bytes=20 * MIB),
        cost_estimate=pl.CostEstimate(
            flops=400_000_000, bytes_accessed=6_400_000, transcendentals=3_200_000
        ),
        name="decode",
    )(first, rest)
    back = lambda a: jnp.swapaxes(a.reshape(experts, width, total), 1, 2)
    return back(ready_g), back(ready_u), scale_g, scale_u


def gathered(block, axis):
    n, held = lax.axis_size(axis), block[None]
    bit = n // 2
    while bit:
        other = lax.ppermute(held, axis, [(i, i ^ bit) for i in range(n)])
        high = (lax.axis_index(axis) & bit) != 0
        low, top = jnp.where(high, other, held), jnp.where(high, held, other)
        held = jnp.stack([low, top], axis=1).reshape(-1, *block.shape)
        bit //= 2
    return held


def per_device(train_gate, other_gate, train_up, other_up, router_weight, router_gain):
    experts = train_gate.shape[0]
    parts = lax.axis_size("fsdp")
    latest = (train_gate, other_gate, train_up, other_up)
    sent = lambda a: lax.all_to_all(a, "fsdp", split_axis=0, concat_axis=0, tiled=True)

    codes, norms = encode_first(parts, *latest, router_weight.T, router_gain[None])
    first = sent(codes)
    rest = sent(encode_rest(parts, *latest, norms))

    router = gathered(first[:, -8:, :], "ep")
    groups, half = router.shape[0], LANES // 2
    router = router.reshape(groups, parts, 8, 2, half).transpose(1, 4, 0, 3, 2)
    serve_router = router.reshape(parts * half, groups * 16)

    return (*decode(experts, first, rest), serve_router)


def solution(mesh):
    in_specs = (
        P("ep", "fsdp", None),
        P("ep", "fsdp", None),
        P("ep", "fsdp", None),
        P("ep", "fsdp", None),
        P("fsdp", "ep"),
        P("fsdp"),
    )
    out_specs = (
        P("ep", None, "fsdp"),
        P("ep", None, "fsdp"),
        P("ep", "fsdp"),
        P("ep", "fsdp"),
        P(),
    )
    return jax.shard_map(
        per_device, mesh=mesh, in_specs=in_specs, out_specs=out_specs, check_vma=False
    )
```

time: 142 us -> 109 us (0.77); the launches traced: 140 us -> 108 us
  waiting for transfers between devices: 87.7 us -> 56.5 us
  starting transfers between devices: 27.2 us -> 19.6 us
  local copies, waits for them, and re-layouts: 4.97 us -> 11.2 us
    ppermute x8 -> x3, waiting for transfers between devices: 87.7 us -> 10.4 us  [gathered(): other = lax.ppermute(held, axis, [(i, i ^ bit) for i in range(n)])]
    all_to_all x1 -> x2, waiting for transfers between devices: 0.01 us -> 46.1 us  [per_device(): lax.all_to_all(a, 'fsdp', split_axis=0, concat_axis=0, tiled=True)]
    ppermute x8 -> x3, starting transfers between devices: 15.6 us -> 2.41 us  [gathered(): other = lax.ppermute(held, axis, [(i, i ^ bit) for i in range(n)])]
    all_to_all x1 -> x2, starting transfers between devices: 11.6 us -> 17.1 us  [per_device(): lax.all_to_all(a, 'fsdp', split_axis=0, concat_axis=0, tiled=True)]
    another operation x6 -> x3, local copies, waits for them, and re-layouts: 0.97 us -> 4.02 us  [the longest x1 3.17 us: per_device(): router = router.reshape(groups, parts, 8, 2, half).transpose(1, 4, 0, 3, 2)]
    reshape x2 -> x1, local copies, waits for them, and re-layouts: 0.26 us -> 2.71 us  [per_device(): serve_router = router.reshape(parts * half, groups * 16)]
    transpose x1, local copies, waits for them, and re-layouts: 0.04 us -> 2.47 us  [per_device(): router = router.reshape(groups, parts, 8, 2, half).transpose(1, 4, 0, 3, 2)]
    unnamed x7 -> x1, local copies, waits for them, and re-layouts: 3.7 us -> 2.04 us
  transfers between devices with their start and end apart: 9 -> 5, of which waited for: 8 -> 5; matrix products, arithmetic and copies ran while one was open for 3% -> 12% of each run, Pallas kernels for 0% -> 8%
where the time goes in v2:
time: 109 us; the launch traced here: 108 us
  waiting for transfers between devices  56.5 us (52%)
  starting transfers between devices  19.6 us (18%)
  Pallas kernels  18.3 us (17%)
  local copies, waits for them, and re-layouts  11.2 us (10%)
  other arithmetic  1.77 us (2%)
    all_to_all x2, waiting for transfers between devices, per_device(): lax.all_to_all(a, 'fsdp', split_axis=0, concat_axis=0, tiled=True)  46.1 us
    all_to_all x2, starting transfers between devices, per_device(): lax.all_to_all(a, 'fsdp', split_axis=0, concat_axis=0, tiled=True)  17.1 us
    ppermute x3, waiting for transfers between devices, gathered(): other = lax.ppermute(held, axis, [(i, i ^ bit) for i in range(n)])  10.4 us
    pallas_call x1, Pallas kernels, encode_rest(): pl.pallas_call(functools.partial(rest_kernel, parts), grid=(steps,), in_s...  8.64 us
    pallas_call x1, Pallas kernels, decode(): pl.pallas_call(decode_kernel, in_specs=[vmem, vmem], out_specs=[anywhere,...  7.08 us
    another operation x1, local copies, waits for them, and re-layouts, per_device(): router = router.reshape(groups, parts, 8, 2, half).transpose(1, 4, 0, 3, 2)  3.17 us
    reshape x1, local copies, waits for them, and re-layouts, per_device(): serve_router = router.reshape(parts * half, groups * 16)  2.71 us
    pallas_call x1, Pallas kernels, encode_first(): pl.pallas_call(functools.partial(first_kernel, parts), grid=(1,), in_spec...  2.53 us
  transfers between devices with their start and end apart: 5, of which 5 were waited for; matrix products, arithmetic and copies ran while one was open for 12% of the time, Pallas kernels for 8%

profile of v2, /device:TPU:22, one launch (start us, length us, event | category | flops | bytes accessed | tf_op | source)
XLA Modules:
  0.0 108.0 jit_solution(2012969772047657447)
XLA Ops:
  0.6 2.5 %encode_first.1 = (bf16[32,56,128]{2,1,0:T(8,128)(2,1)}, f32[8,768]{1,0:T(8,128)}) custom-call(f32[16,64,768]{2,1,0:T(8,128)} %tg.3, bf16[16,64,768]{2,1,0:T(8,128)(2,1)} %og.3, f32[16,64,768]{2,1,0:T(8,128)} %tu.3, bf16[16,64,768]{2,1,0:T(8,128)(2,1)} %ou.3, f32[16,64]{1,0:T(8,128)} %bitcast.44, f32[1,64]{1,0:T(1,128)} %bitcast.45), custom_call_target="tpu_custom_call" | custom-call | flops 50000000 | bytes 1700000 | tf_op jit(solution)/shard_map/encode_first/pallas_call | solution.py:58
  3.2 11.6 %all-to-all-start = ((bf16[32,56,128]{2,1,0:T(8,128)(2,1)}), bf16[32,56,128]{2,1,0:T(8,128)(2,1)S(1)}, u32[]{:S(2)}, u32[]{:S(2)}) async-start(bf16[32,56,128]{2,1,0:T(8,128)(2,1)} %get-tuple-element.11), calls=%async_computation | async-start | bytes 917504 | tf_op jit(solution)/shard_map/all_to_all | solution.py:275
  14.8 8.6 %encode_rest.1 = bf16[32,344,128]{2,1,0:T(8,128)(2,1)} custom-call(f32[16,64,768]{2,1,0:T(8,128)} %tg.3, bf16[16,64,768]{2,1,0:T(8,128)(2,1)} %og.3, f32[16,64,768]{2,1,0:T(8,128)} %tu.3, bf16[16,64,768]{2,1,0:T(8,128)(2,1)} %ou.3, f32[8,768]{1,0:T(8,128)} %get-tuple-element.12.before), custom_call_target="tpu_custom_call" | custom-call | flops 400000000 | bytes 11000000 | tf_op jit(solution)/shard_map/encode_rest/pallas_call | solution.py:122
  23.4 6.8 %all-to-all-done.first = bf16[32,56,128]{2,1,0:T(8,128)(2,1)S(1)} async-done(((bf16[32,56,128]{2,1,0:T(8,128)(2,1)}), bf16[32,56,128]{2,1,0:T(8,128)(2,1)S(1)}, u32[]{:S(2)}, u32[]{:S(2)}) %all-to-all-start) | async-done | bytes 458784 | tf_op jit(solution)/shard_map/all_to_all | solution.py:275
  30.2 5.6 %all-to-all-start.1 = ((bf16[32,344,128]{2,1,0:T(8,128)(2,1)}), bf16[32,344,128]{2,1,0:T(8,128)(2,1)S(1)}, u32[]{:S(2)}, u32[]{:S(2)}) async-start(bf16[32,344,128]{2,1,0:T(8,128)(2,1)} %encode_rest.1), calls=%async_computation.1 | async-start | bytes 5636096 | tf_op jit(solution)/shard_map/all_to_all | solution.py:275
  35.8 1.5 %collective-permute-start = (bf16[1,32,8,128]{3,2,1,0:T(8,128)(2,1)S(1)}, bf16[1,32,8,128]{3,2,1,0:T(8,128)(2,1)S(1)}, u32[]{:S(2)}, u32[]{:S(2)}) collective-permute-start(bf16[1,32,8,128]{3,2,1,0:T(8,128)(2,1)S(1)} %slice_bitcast_fusion), channel_id=1, source_target_pairs={{0,128},{32,160},{64,192},{96,224},{128,0},{160,32},{192,64},{224,... | collective-permute-start | bytes 196616 | tf_op jit(solution)/shard_map/ppermute | solution.py:263
  37.3 4.4 %collective-permute-done = bf16[1,32,8,128]{3,2,1,0:T(8,128)(2,1)S(1)} collective-permute-done((bf16[1,32,8,128]{3,2,1,0:T(8,128)(2,1)S(1)}, bf16[1,32,8,128]{3,2,1,0:T(8,128)(2,1)S(1)}, u32[]{:S(2)}, u32[]{:S(2)}) %collective-permute-start) | collective-permute-done | bytes 65568 | tf_op jit(solution)/shard_map/ppermute | solution.py:263
  41.6 0.7 maximum_bitcast_fusion
  42.3 0.8 collective-permute-start.1
  43.1 4.3 %collective-permute-done.1 = bf16[2,32,8,128]{3,2,1,0:T(8,128)(2,1)S(1)} collective-permute-done((bf16[2,32,8,128]{3,2,1,0:T(8,128)(2,1)}, bf16[2,32,8,128]{3,2,1,0:T(8,128)(2,1)S(1)}, u32[]{:S(2)}, u32[]{:S(2)}) %collective-permute-start.1) | collective-permute-done | bytes 131104 | tf_op jit(solution)/shard_map/ppermute | solution.py:263
  47.6 0.1 collective-permute-start.2
  47.7 1.6 %collective-permute-done.2 = bf16[4,32,8,128]{3,2,1,0:T(8,128)(2,1)} collective-permute-done((bf16[4,32,8,128]{3,2,1,0:T(8,128)(2,1)S(1)}, bf16[4,32,8,128]{3,2,1,0:T(8,128)(2,1)}, u32[]{:S(2)}, u32[]{:S(2)}) %collective-permute-start.2) | collective-permute-done | bytes 262176 | tf_op jit(solution)/shard_map/ppermute | solution.py:263
  49.3 1.0 select_bitcast_fusion.1
  50.3 0.1 pad_maximum_fusion
  50.4 0.8 copy.12
  51.2 3.2 %reshape_reshape.3 = bf16[8,32,8,2,64]{4,3,2,1,0:T(2,128)(2,1)} reshape(bf16[4,2,32,8,128]{4,3,2,1,0:T(8,128)(2,1)} %copy.12) | data formatting | bytes 1048576 | tf_op jit(solution)/shard_map/reshape;reshape | solution.py:283
  54.4 2.5 %copy.13 = bf16[32,64,8,2,8]{1,0,4,3,2:T(8,128)(2,1)} copy(bf16[32,64,8,2,8]{1,3,4,0,2:T(2,128)(2,1)} %bitcast.42) | data formatting | bytes 1048576 | tf_op jit(solution)/shard_map/transpose | solution.py:283
  56.9 2.7 %reshape.29 = bf16[2048,128]{0,1:T(8,128)(2,1)} reshape(bf16[32,64,8,2,8]{1,0,4,3,2:T(8,128)(2,1)} %copy.13) | data formatting | bytes 1048576 | tf_op jit(solution)/shard_map/reshape | solution.py:284
  59.6 2.0 %copy.14 = bf16[2048,128]{1,0:T(8,128)(2,1)} copy(bf16[2048,128]{0,1:T(8,128)(2,1)} %reshape.29) | data formatting | bytes 1048576
  61.6 39.3 %all-to-all-done.1.rest = bf16[32,344,128]{2,1,0:T(8,128)(2,1)S(1)} async-done(((bf16[32,344,128]{2,1,0:T(8,128)(2,1)}), bf16[32,344,128]{2,1,0:T(8,128)(2,1)S(1)}, u32[]{:S(2)}, u32[]{:S(2)}) %all-to-all-start.1) | async-done | bytes 2818080 | tf_op jit(solution)/shard_map/all_to_all | solution.py:275
  100.9 7.1 %decode.1 = (bf16[384,2048]{1,0:T(8,128)(2,1)}, bf16[384,2048]{1,0:T(8,128)(2,1)}, f32[16,24]{1,0:T(8,128)}, f32[16,24]{1,0:T(8,128)}) custom-call(bf16[32,56,128]{2,1,0:T(8,128)(2,1)S(1)} %all-to-all-done.first, bf16[32,344,128]{2,1,0:T(8,128)(2,1)S(1)} %all-to-all-done.1.rest), custom_call_target="tpu_custom_call" | custom-call | flops 400000000 | bytes 6400000 | tf_op jit(solution)/shard_map/decode/pallas_call | solution.py:236
  (5 shorter events, 0.1 us)
Async XLA Ops:
  3.2 27.0 %all-to-all-start = ((bf16[32,56,128]{2,1,0:T(8,128)(2,1)}), bf16[32,56,128]{2,1,0:T(8,128)(2,1)S(1)}, u32[]{:S(2)}, u32[]{:S(2)}) async-start(bf16[32,56,128]{2,1,0:T(8,128)(2,1)} %get-tuple-element.11), calls=%async_computation | async-start | bytes 917504 | tf_op jit(solution)/shard_map/all_to_all | solution.py:275
  30.2 70.8 %all-to-all-start.1 = ((bf16[32,344,128]{2,1,0:T(8,128)(2,1)}), bf16[32,344,128]{2,1,0:T(8,128)(2,1)S(1)}, u32[]{:S(2)}, u32[]{:S(2)}) async-start(bf16[32,344,128]{2,1,0:T(8,128)(2,1)} %encode_rest.1), calls=%async_computation.1 | async-start | bytes 5636096 | tf_op jit(solution)/shard_map/all_to_all | solution.py:275
  35.8 5.9 %collective-permute-start = (bf16[1,32,8,128]{3,2,1,0:T(8,128)(2,1)S(1)}, bf16[1,32,8,128]{3,2,1,0:T(8,128)(2,1)S(1)}, u32[]{:S(2)}, u32[]{:S(2)}) collective-permute-start(bf16[1,32,8,128]{3,2,1,0:T(8,128)(2,1)S(1)} %slice_bitcast_fusion), channel_id=1, source_target_pairs={{0,128},{32,160},{64,192},{96,224},{128,0},{160,32},{192,64},{224,... | collective-permute-start | bytes 196616 | tf_op jit(solution)/shard_map/ppermute | solution.py:263
  42.3 5.2 %collective-permute-start.1 = (bf16[2,32,8,128]{3,2,1,0:T(8,128)(2,1)}, bf16[2,32,8,128]{3,2,1,0:T(8,128)(2,1)S(1)}, u32[]{:S(2)}, u32[]{:S(2)}) collective-permute-start(bf16[2,32,8,128]{3,2,1,0:T(8,128)(2,1)} %maximum_bitcast_fusion), channel_id=1, source_target_pairs={{0,64},{32,96},{64,0},{96,32},{128,192},{160,224},{192,128},{224,1... | collective-permute-start | bytes 393224 | tf_op jit(solution)/shard_map/ppermute | solution.py:263
  47.6 1.8 %collective-permute-start.2 = (bf16[4,32,8,128]{3,2,1,0:T(8,128)(2,1)S(1)}, bf16[4,32,8,128]{3,2,1,0:T(8,128)(2,1)}, u32[]{:S(2)}, u32[]{:S(2)}) collective-permute-start(bf16[4,32,8,128]{3,2,1,0:T(8,128)(2,1)S(1)} %bitcast.43), channel_id=1, source_target_pairs={{0,32},{32,0},{64,96},{96,64},{128,160},{160,128},{192,224},{224,1... | collective-permute-start | bytes 786440 | tf_op jit(solution)/shard_map/ppermute | solution.py:263

commit v3 on v2

v3 whole, which is shorter than its diff:
```python
import functools

import jax
import jax.numpy as jnp
from jax import lax
from jax.experimental import pallas as pl
from jax.experimental.pallas import tpu as pltpu
from jax.sharding import PartitionSpec as P

POWER = 15
SPREAD = 5.0
LEAST = 1e-30
SMALLEST = 2.0**-126
PAIR = 2
LANES = 128
MIB = 2**20


def coded(latest):
    mean = jnp.sum(jnp.abs(latest), axis=0, keepdims=True) * (1.0 / (latest.shape[0] * SPREAD))
    norm = jnp.maximum(mean, LEAST).astype(jnp.bfloat16).astype(jnp.float32)
    v = latest * (1.0 / norm)
    v2 = v * v
    v4 = v2 * v2
    v8 = v4 * v4
    return (v8 * v4) * (v2 * v), norm


def coded_expert(parts, tg, og, tu, ou):
    cg, ng = coded(tg[...] + og[...].astype(jnp.float32))
    cu, nu = coded(tu[...] + ou[...].astype(jnp.float32))
    return jnp.concatenate([cg, cu], axis=0).T.reshape(parts, -1, LANES), ng, nu


def first_kernel(parts, tg, og, tu, ou, weight, gain, out, norms):
    width = tg.shape[2] // parts
    norms[...] = jnp.zeros_like(norms)
    part = weight[...] * gain[...]
    part = jnp.concatenate([part[:8], part[8:]], axis=1).astype(jnp.bfloat16)
    out[:, width:, :] = jnp.broadcast_to(part[None], (parts, 8, LANES))
    codes, norms[0:1, :], norms[1:2, :] = coded_expert(
        parts, *(a.at[0] for a in (tg, og, tu, ou))
    )
    for k in range(0, width, 8):
        out[:, k : k + 8, :] = codes[:, k : k + 8].astype(jnp.bfloat16)


def encode_first(parts, tg, og, tu, ou, weight, gain):
    _, mine, columns = tg.shape
    width = columns // parts
    block = lambda: pl.BlockSpec((1, mine, columns), lambda s: (0, 0, 0))
    whole = lambda a: pl.BlockSpec(a.shape, lambda s: (0,) * len(a.shape))
    out = jax.ShapeDtypeStruct((parts, width + 8, LANES), jnp.bfloat16)
    norms = jax.ShapeDtypeStruct((8, columns), jnp.float32)
    return pl.pallas_call(
        functools.partial(first_kernel, parts),
        grid=(1,),
        in_specs=[block() for _ in range(4)] + [whole(weight), whole(gain)],
        out_specs=[whole(out), whole(norms)],
        out_shape=[out, norms],
        cost_estimate=pl.CostEstimate(flops=25_000_000, bytes_accessed=900_000, transcendentals=0),
        name="encode_first",
    )(tg, og, tu, ou, weight, gain)


def rest_kernel(parts, tg, og, tu, ou, before, out, ins, codes, norms, norm_rows, in_sems, sems, norm_sem):
    count = codes.shape[0]
    width = codes.shape[2]

    def reads(e):
        return [
            pltpu.make_async_copy(a.at[e + 1], held.at[e], in_sems.at[e, m])
            for m, (a, held) in enumerate(zip((tg, og, tu, ou), ins))
        ]

    def copy(e):
        return pltpu.make_async_copy(
            codes.at[e], out.at[:, pl.ds(pl.multiple_of(e * width, 8), width), :], sems.at[e]
        )

    @pl.loop(0, count)
    def _(e):
        for read in reads(e):
            read.start()

    norms[...] = jnp.zeros_like(norms)
    norms[0:8, :] = before[...]

    @pl.loop(0, count)
    def _(e):
        for read in reads(e):
            read.wait()
        turned, ng, nu = coded_expert(parts, *(held.at[e] for held in ins))
        for k in range(0, width, 8):
            codes[e, :, k : k + 8, :] = turned[:, k : k + 8].astype(jnp.bfloat16)
        norms[pl.ds(2 * e + 2, 1), :] = ng
        norms[pl.ds(2 * e + 3, 1), :] = nu
        copy(e).start()

    turned = norms[...].T.reshape(parts, width // 8, 8, LANES)
    packed = turned[:, 0]
    for k in range(1, width // 8):
        packed = packed + pltpu.roll(turned[:, k], 32 * k, 2)
    norm_rows[...] = packed.astype(jnp.bfloat16)
    last = pltpu.make_async_copy(norm_rows, out.at[:, pl.ds(count * width, 8), :], norm_sem)
    last.start()

    @pl.loop(0, count)
    def _(e):
        copy(e).wait()

    last.wait()


def encode_rest(parts, tg, og, tu, ou, before):
    experts, mine, columns = tg.shape
    width = columns // parts
    count = experts - 1
    vmem, anywhere = pl.BlockSpec(memory_space=pltpu.VMEM), pl.BlockSpec(memory_space=pl.ANY)

    def kernel(tg, og, tu, ou, before, out, a, b, c, d, *scratch):
        rest_kernel(parts, tg, og, tu, ou, before, out, (a, b, c, d), *scratch)

    return pl.pallas_call(
        kernel,
        in_specs=[anywhere] * 4 + [vmem],
        out_specs=anywhere,
        out_shape=jax.ShapeDtypeStruct((parts, count * width + 8, LANES), jnp.bfloat16),
        scratch_shapes=[
            *[pltpu.VMEM((count, mine, columns), a.dtype) for a in (tg, og, tu, ou)],
            pltpu.VMEM((count, parts, width, LANES), jnp.bfloat16),
            pltpu.VMEM((LANES, columns), jnp.float32),
            pltpu.VMEM((parts, 8, LANES), jnp.bfloat16),
            pltpu.SemaphoreType.DMA((count, 4)),
            pltpu.SemaphoreType.DMA((count,)),
            pltpu.SemaphoreType.DMA,
        ],
        cost_estimate=pl.CostEstimate(flops=400_000_000, bytes_accessed=11_000_000, transcendentals=0),
        name="encode_rest",
    )(tg, og, tu, ou, before)


def decode_kernel(
    first, rest, out_g, out_u, scale_g, scale_u, pick, sums, ready, sems, scales, scale_sems, *pairs
):
    spreads, values, factors = pairs[0:2], pairs[2:4], pairs[4:6]
    parts = first.shape[0]
    width = first.shape[1] - 8
    rows = width * PAIR
    tiles = width // 8
    steps = (rest.shape[1] - 8 + width) // rows
    total = parts * LANES // 2
    half = LANES // 2
    lane = lax.broadcasted_iota(jnp.int32, (8, LANES), 1)
    left = lane < half
    sums[...] = jnp.zeros_like(sums)

    source = lax.broadcasted_iota(jnp.int32, pick.shape, 0)
    goal = lax.broadcasted_iota(jnp.int32, pick.shape, 1)
    tile, at = goal // LANES, goal % LANES
    wanted = 32 * (tile % tiles) + 2 * (tile // tiles) + at // half
    pick[...] = (source == wanted).astype(jnp.bfloat16)

    def copies(step, slot):
        where = pl.ds(pl.multiple_of(step * rows, rows), rows)
        return [
            pltpu.make_async_copy(ready.at[slot, m], out.at[where, :], sems.at[slot, m])
            for m, out in enumerate((out_g, out_u))
        ]

    def spread_norms(step, side):
        norm = rest[:, steps * rows - width :, :].reshape(parts * 8, LANES).astype(jnp.float32)
        norm = pltpu.roll(norm, lax.rem(LANES - 2 * PAIR * step, LANES), 1)
        spreads[side][...] = jnp.dot(
            norm.astype(jnp.bfloat16), pick[...], preferred_element_type=jnp.float32
        )

    def read(step, side, codes_of):
        acc = [jnp.zeros((8, LANES), jnp.float32) for _ in range(PAIR * tiles)]
        for src in range(parts):
            whole = codes_of(src).astype(jnp.float32)
            for k in range(PAIR * tiles):
                c = whole[8 * k : 8 * k + 8]
                scale = spreads[side][src * 8 : src * 8 + 8, k * LANES : (k + 1) * LANES]
                size = jnp.log2(jnp.maximum(jnp.abs(c), SMALLEST))
                value = (c * scale) * jnp.exp2(size * (1.0 / POWER - 1.0))
                acc[k] = acc[k] + jnp.abs(value)
                values[side][src, 8 * k : 8 * k + 8, :] = value
        for k in range(PAIR * tiles):
            at = slice(8 * k, 8 * k + 8)
            sg = jnp.sum(jnp.where(left, acc[k], 0.0), axis=1, keepdims=True) * (1.0 / total)
            su = jnp.sum(jnp.where(left, 0.0, acc[k]), axis=1, keepdims=True) * (1.0 / total)
            sums[at, :] += jnp.where(
                lane == 2 * step, sg, jnp.where(lane == 2 * step + 1, su, 0.0)
            )
            factors[side][at, :] = 1.0 / jnp.where(left, sg, su)

    def write(step, side):
        for t in range(parts // 2):
            for k in range(PAIR * tiles):
                at = slice(8 * k, 8 * k + 8)
                factor = factors[side][at, :]
                even = values[side][2 * t, at, :] * factor
                odd = values[side][2 * t + 1, at, :] * factor
                g = jnp.where(left, even, pltpu.roll(odd, half, 1))
                u = jnp.where(left, pltpu.roll(even, half, 1), odd)
                for m, whole in enumerate((g, u)):
                    ready[side, m, at, t * LANES : (t + 1) * LANES] = whole.astype(jnp.bfloat16)
        for copy in copies(step, side):
            copy.start()

    def wait(step, side):
        for copy in copies(step, side):
            copy.wait()

    def from_rest(step, side):
        start = pl.multiple_of(step * rows - width, 8)
        read(step, side, lambda src: rest[src, pl.ds(start, rows), :])

    spread_norms(jnp.int32(0), 0)
    spread_norms(jnp.int32(1), 1)
    read(
        jnp.int32(0),
        0,
        lambda src: jnp.concatenate([first[src, :width, :], rest[src, :width, :]], axis=0),
    )

    @pl.loop(0, steps // 2 - 1)
    def _(i):
        for side in (1, 0):
            step = 2 * i + 2 - side

            @pl.when(i > 0)
            def _():
                wait(step - 3, 1 - side)

            write(step - 1, 1 - side)
            spread_norms(step + 1, 1 - side)
            from_rest(step, side)

    last = steps - 1
    wait(last - 3, 0)
    write(last - 1, 0)
    from_rest(jnp.int32(last), 1)
    turned = jnp.concatenate(
        [sums[...], jnp.zeros((LANES - rows, LANES), jnp.float32)], axis=0
    ).T
    turned = turned[: 2 * steps].reshape(steps, 2, LANES)
    scale_copies = []
    for m, out in enumerate((scale_g, scale_u)):
        for p in range(PAIR):
            scales[m, pl.ds(p, steps, stride=PAIR), :] = turned[:, m, p * width : (p + 1) * width]
        scale_copies.append(pltpu.make_async_copy(scales.at[m], out, scale_sems.at[m]))
        scale_copies[m].start()
    wait(last - 2, 1)
    write(last, 1)
    wait(last - 1, 0)
    wait(last, 1)
    for copy in scale_copies:
        copy.wait()


def decode(experts, first, rest):
    parts, rows, lanes = first.shape
    width = rows - 8
    rows = width * PAIR
    total = parts * lanes // 2
    ready = jax.ShapeDtypeStruct((experts * width, total), jnp.bfloat16)
    scale = jax.ShapeDtypeStruct((experts, width), jnp.float32)
    vmem, anywhere = pl.BlockSpec(memory_space=pltpu.VMEM), pl.BlockSpec(memory_space=pl.ANY)
    ready_g, ready_u, scale_g, scale_u = pl.pallas_call(
        decode_kernel,
        in_specs=[vmem, vmem],
        out_specs=[anywhere] * 4,
        out_shape=[ready, ready, scale, scale],
        scratch_shapes=[
            pltpu.VMEM((lanes, rows // 8 * lanes), jnp.bfloat16),
            pltpu.VMEM((rows, lanes), jnp.float32),
            pltpu.VMEM((2, 2, rows, total), jnp.bfloat16),
            pltpu.SemaphoreType.DMA((2, 2)),
            pltpu.VMEM((2, experts, width), jnp.float32),
            pltpu.SemaphoreType.DMA((2,)),
            *[pltpu.VMEM((parts * 8, rows // 8 * lanes), jnp.float32)] * 2,
            *[pltpu.VMEM((parts, rows, lanes), jnp.float32)] * 2,
            *[pltpu.VMEM((rows, lanes), jnp.float32)] * 2,
        ],
        compiler_params=pltpu.CompilerParams(vmem_limit_bytes=20 * MIB),
        cost_estimate=pl.CostEstimate(
            flops=400_000_000, bytes_accessed=6_400_000, transcendentals=3_200_000
        ),
        name="decode",
    )(first, rest)
    back = lambda a: jnp.swapaxes(a.reshape(experts, width, total), 1, 2)
    return back(ready_g), back(ready_u), scale_g, scale_u


def gathered(block, axis):
    n, held = lax.axis_size(axis), block[None]
    bit = n // 2
    while bit:
        other = lax.ppermute(held, axis, [(i, i ^ bit) for i in range(n)])
        high = (lax.axis_index(axis) & bit) != 0
        low, top = jnp.where(high, other, held), jnp.where(high, held, other)
        held = jnp.stack([low, top], axis=1).reshape(-1, *block.shape)
        bit //= 2
    return held


def per_device(train_gate, other_gate, train_up, other_up, router_weight, router_gain):
    experts = train_gate.shape[0]
    parts = lax.axis_size("fsdp")
    latest = (train_gate, other_gate, train_up, other_up)
    sent = lambda a: lax.all_to_all(a, "fsdp", split_axis=0, concat_axis=0, tiled=True)

    codes, norms = encode_first(parts, *latest, router_weight.T, router_gain[None])
    first = sent(codes)
    rest = sent(encode_rest(parts, *latest, norms))

    router = gathered(first[:, -8:, :], "ep")
    groups, half = router.shape[0], LANES // 2
    router = router.reshape(groups, parts, 8, 2, half).transpose(1, 4, 0, 3, 2)
    serve_router = router.reshape(parts * half, groups * 16)

    return (*decode(experts, first, rest), serve_router)


def solution(mesh):
    in_specs = (
        P("ep", "fsdp", None),
        P("ep", "fsdp", None),
        P("ep", "fsdp", None),
        P("ep", "fsdp", None),
        P("fsdp", "ep"),
        P("fsdp"),
    )
    out_specs = (
        P("ep", None, "fsdp"),
        P("ep", None, "fsdp"),
        P("ep", "fsdp"),
        P("ep", "fsdp"),
        P(),
    )
    return jax.shard_map(
        per_device, mesh=mesh, in_specs=in_specs, out_specs=out_specs, check_vma=False
    )
```

time: 109 us -> 107 us (0.982)
  Pallas kernels: 18.3 us -> 15.3 us
    pallas_call x2, Pallas kernels: 15.7 us -> 13.2 us  [the longest x1 7.3 us: encode_rest(): pl.pallas_call(kernel, in_specs=[anywhere] * 4 + [vmem], out_specs=anywhe...]
  transfers between devices with their start and end apart: 5 -> 5, of which waited for: 5 -> 5; matrix products, arithmetic and copies ran while one was open for 12% -> 12% of each run, Pallas kernels for 8% -> 7%
where the time goes in v3:
time: 107 us; the launch traced here: 106 us
  waiting for transfers between devices  56.9 us (53%)
  starting transfers between devices  19.9 us (19%)
  Pallas kernels  15.3 us (14%)
  local copies, waits for them, and re-layouts  11.2 us (10%)
  other arithmetic  1.77 us (2%)
    all_to_all x2, waiting for transfers between devices, per_device(): lax.all_to_all(a, 'fsdp', split_axis=0, concat_axis=0, tiled=True)  46.5 us
    all_to_all x2, starting transfers between devices, per_device(): lax.all_to_all(a, 'fsdp', split_axis=0, concat_axis=0, tiled=True)  17.5 us
    ppermute x3, waiting for transfers between devices, gathered(): other = lax.ppermute(held, axis, [(i, i ^ bit) for i in range(n)])  10.4 us
    pallas_call x1, Pallas kernels, encode_rest(): pl.pallas_call(kernel, in_specs=[anywhere] * 4 + [vmem], out_specs=anywhe...  7.3 us
    pallas_call x1, Pallas kernels, decode(): pl.pallas_call(decode_kernel, in_specs=[vmem, vmem], out_specs=[anywhere]...  5.93 us
    another operation x1, local copies, waits for them, and re-layouts, per_device(): router = router.reshape(groups, parts, 8, 2, half).transpose(1, 4, 0, 3, 2)  3.17 us
    reshape x1, local copies, waits for them, and re-layouts, per_device(): serve_router = router.reshape(parts * half, groups * 16)  2.71 us
    transpose x1, local copies, waits for them, and re-layouts, per_device(): router = router.reshape(groups, parts, 8, 2, half).transpose(1, 4, 0, 3, 2)  2.47 us
  transfers between devices with their start and end apart: 5, of which 5 were waited for; matrix products, arithmetic and copies ran while one was open for 12% of the time, Pallas kernels for 7%

profile of v3, /device:TPU:22, one launch (start us, length us, event | category | flops | bytes accessed | tf_op | source)
XLA Modules:
  0.0 105.8 jit_solution(1126477644196529752)
XLA Ops:
  0.6 2.1 %encode_first.1 = (bf16[32,32,128]{2,1,0:T(8,128)(2,1)}, f32[8,768]{1,0:T(8,128)}) custom-call(f32[16,64,768]{2,1,0:T(8,128)} %tg.3, bf16[16,64,768]{2,1,0:T(8,128)(2,1)} %og.3, f32[16,64,768]{2,1,0:T(8,128)} %tu.3, bf16[16,64,768]{2,1,0:T(8,128)(2,1)} %ou.3, f32[16,64]{1,0:T(8,128)} %bitcast.44, f32[1,64]{1,0:T(1,128)} %bitcast.45), custom_call_target="tpu_custom_call" | custom-call | flops 25000000 | bytes 900000 | tf_op jit(solution)/shard_map/encode_first/pallas_call | solution.py:55
  2.7 11.6 %all-to-all-start = ((bf16[32,32,128]{2,1,0:T(8,128)(2,1)}), bf16[32,32,128]{2,1,0:T(8,128)(2,1)S(1)}, u32[]{:S(2)}, u32[]{:S(2)}) async-start(bf16[32,32,128]{2,1,0:T(8,128)(2,1)} %get-tuple-element.11), calls=%async_computation | async-start | bytes 524288 | tf_op jit(solution)/shard_map/all_to_all | solution.py:313
  14.3 7.3 %encode_rest.1 = bf16[32,368,128]{2,1,0:T(8,128)(2,1)} custom-call(f32[16,64,768]{2,1,0:T(8,128)} %tg.3, bf16[16,64,768]{2,1,0:T(8,128)(2,1)} %og.3, f32[16,64,768]{2,1,0:T(8,128)} %tu.3, bf16[16,64,768]{2,1,0:T(8,128)(2,1)} %ou.3, f32[8,768]{1,0:T(8,128)} %get-tuple-element.12.before), custom_call_target="tpu_custom_call" | custom-call | flops 400000000 | bytes 11000000 | tf_op jit(solution)/shard_map/encode_rest/pallas_call | solution.py:124
  21.6 3.9 %all-to-all-done.first = bf16[32,32,128]{2,1,0:T(8,128)(2,1)S(1)} async-done(((bf16[32,32,128]{2,1,0:T(8,128)(2,1)}), bf16[32,32,128]{2,1,0:T(8,128)(2,1)S(1)}, u32[]{:S(2)}, u32[]{:S(2)}) %all-to-all-start) | async-done | bytes 262176 | tf_op jit(solution)/shard_map/all_to_all | solution.py:313
  25.5 5.9 %all-to-all-start.1 = ((bf16[32,368,128]{2,1,0:T(8,128)(2,1)}), bf16[32,368,128]{2,1,0:T(8,128)(2,1)S(1)}, u32[]{:S(2)}, u32[]{:S(2)}) async-start(bf16[32,368,128]{2,1,0:T(8,128)(2,1)} %encode_rest.1), calls=%async_computation.1 | async-start | bytes 6029312 | tf_op jit(solution)/shard_map/all_to_all | solution.py:313
  31.4 1.5 %collective-permute-start = (bf16[1,32,8,128]{3,2,1,0:T(8,128)(2,1)S(1)}, bf16[1,32,8,128]{3,2,1,0:T(8,128)(2,1)S(1)}, u32[]{:S(2)}, u32[]{:S(2)}) collective-permute-start(bf16[1,32,8,128]{3,2,1,0:T(8,128)(2,1)S(1)} %slice_bitcast_fusion), channel_id=1, source_target_pairs={{0,128},{32,160},{64,192},{96,224},{128,0},{160,32},{192,64},{224,... | collective-permute-start | bytes 196616 | tf_op jit(solution)/shard_map/ppermute | solution.py:301
  32.9 4.4 %collective-permute-done = bf16[1,32,8,128]{3,2,1,0:T(8,128)(2,1)S(1)} collective-permute-done((bf16[1,32,8,128]{3,2,1,0:T(8,128)(2,1)S(1)}, bf16[1,32,8,128]{3,2,1,0:T(8,128)(2,1)S(1)}, u32[]{:S(2)}, u32[]{:S(2)}) %collective-permute-start) | collective-permute-done | bytes 65568 | tf_op jit(solution)/shard_map/ppermute | solution.py:301
  37.3 0.7 maximum_bitcast_fusion
  38.0 0.8 collective-permute-start.1
  38.8 4.3 %collective-permute-done.1 = bf16[2,32,8,128]{3,2,1,0:T(8,128)(2,1)S(1)} collective-permute-done((bf16[2,32,8,128]{3,2,1,0:T(8,128)(2,1)}, bf16[2,32,8,128]{3,2,1,0:T(8,128)(2,1)S(1)}, u32[]{:S(2)}, u32[]{:S(2)}) %collective-permute-start.1) | collective-permute-done | bytes 131104 | tf_op jit(solution)/shard_map/ppermute | solution.py:301
  43.2 0.1 collective-permute-start.2
  43.3 1.6 %collective-permute-done.2 = bf16[4,32,8,128]{3,2,1,0:T(8,128)(2,1)} collective-permute-done((bf16[4,32,8,128]{3,2,1,0:T(8,128)(2,1)S(1)}, bf16[4,32,8,128]{3,2,1,0:T(8,128)(2,1)}, u32[]{:S(2)}, u32[]{:S(2)}) %collective-permute-start.2) | collective-permute-done | bytes 262176 | tf_op jit(solution)/shard_map/ppermute | solution.py:301
  45.0 1.0 select_bitcast_fusion.1
  46.0 0.1 pad_maximum_fusion
  46.1 0.8 copy.12
  46.9 3.2 %reshape_reshape.3 = bf16[8,32,8,2,64]{4,3,2,1,0:T(2,128)(2,1)} reshape(bf16[4,2,32,8,128]{4,3,2,1,0:T(8,128)(2,1)} %copy.12) | data formatting | bytes 1048576 | tf_op jit(solution)/shard_map/reshape;reshape | solution.py:321
  50.1 2.5 %copy.13 = bf16[32,64,8,2,8]{1,0,4,3,2:T(8,128)(2,1)} copy(bf16[32,64,8,2,8]{1,3,4,0,2:T(2,128)(2,1)} %bitcast.42) | data formatting | bytes 1048576 | tf_op jit(solution)/shard_map/transpose | solution.py:321
  52.5 2.7 %reshape.29 = bf16[2048,128]{0,1:T(8,128)(2,1)} reshape(bf16[32,64,8,2,8]{1,0,4,3,2:T(8,128)(2,1)} %copy.13) | data formatting | bytes 1048576 | tf_op jit(solution)/shard_map/reshape | solution.py:322
  55.2 2.0 %copy.14 = bf16[2048,128]{1,0:T(8,128)(2,1)} copy(bf16[2048,128]{0,1:T(8,128)(2,1)} %reshape.29) | data formatting | bytes 1048576
  57.3 42.6 %all-to-all-done.1.rest = bf16[32,368,128]{2,1,0:T(8,128)(2,1)S(1)} async-done(((bf16[32,368,128]{2,1,0:T(8,128)(2,1)}), bf16[32,368,128]{2,1,0:T(8,128)(2,1)S(1)}, u32[]{:S(2)}, u32[]{:S(2)}) %all-to-all-start.1) | async-done | bytes 3014688 | tf_op jit(solution)/shard_map/all_to_all | solution.py:313
  99.9 5.9 %decode.1 = (bf16[384,2048]{1,0:T(8,128)(2,1)}, bf16[384,2048]{1,0:T(8,128)(2,1)}, f32[16,24]{1,0:T(8,128)}, f32[16,24]{1,0:T(8,128)}) custom-call(bf16[32,32,128]{2,1,0:T(8,128)(2,1)S(1)} %all-to-all-done.first, bf16[32,368,128]{2,1,0:T(8,128)(2,1)S(1)} %all-to-all-done.1.rest), custom_call_target="tpu_custom_call" | custom-call | flops 400000000 | bytes 6400000 | tf_op jit(solution)/shard_map/decode/pallas_call | solution.py:271
  (5 shorter events, 0.1 us)
Async XLA Ops:
  2.7 22.8 %all-to-all-start = ((bf16[32,32,128]{2,1,0:T(8,128)(2,1)}), bf16[32,32,128]{2,1,0:T(8,128)(2,1)S(1)}, u32[]{:S(2)}, u32[]{:S(2)}) async-start(bf16[32,32,128]{2,1,0:T(8,128)(2,1)} %get-tuple-element.11), calls=%async_computation | async-start | bytes 524288 | tf_op jit(solution)/shard_map/all_to_all | solution.py:313
  25.5 74.4 %all-to-all-start.1 = ((bf16[32,368,128]{2,1,0:T(8,128)(2,1)}), bf16[32,368,128]{2,1,0:T(8,128)(2,1)S(1)}, u32[]{:S(2)}, u32[]{:S(2)}) async-start(bf16[32,368,128]{2,1,0:T(8,128)(2,1)} %encode_rest.1), calls=%async_computation.1 | async-start | bytes 6029312 | tf_op jit(solution)/shard_map/all_to_all | solution.py:313
  31.4 5.9 %collective-permute-start = (bf16[1,32,8,128]{3,2,1,0:T(8,128)(2,1)S(1)}, bf16[1,32,8,128]{3,2,1,0:T(8,128)(2,1)S(1)}, u32[]{:S(2)}, u32[]{:S(2)}) collective-permute-start(bf16[1,32,8,128]{3,2,1,0:T(8,128)(2,1)S(1)} %slice_bitcast_fusion), channel_id=1, source_target_pairs={{0,128},{32,160},{64,192},{96,224},{128,0},{160,32},{192,64},{224,... | collective-permute-start | bytes 196616 | tf_op jit(solution)/shard_map/ppermute | solution.py:301
  38.0 5.2 %collective-permute-start.1 = (bf16[2,32,8,128]{3,2,1,0:T(8,128)(2,1)}, bf16[2,32,8,128]{3,2,1,0:T(8,128)(2,1)S(1)}, u32[]{:S(2)}, u32[]{:S(2)}) collective-permute-start(bf16[2,32,8,128]{3,2,1,0:T(8,128)(2,1)} %maximum_bitcast_fusion), channel_id=1, source_target_pairs={{0,64},{32,96},{64,0},{96,32},{128,192},{160,224},{192,128},{224,1... | collective-permute-start | bytes 393224 | tf_op jit(solution)/shard_map/ppermute | solution.py:301
  43.2 1.8 %collective-permute-start.2 = (bf16[4,32,8,128]{3,2,1,0:T(8,128)(2,1)S(1)}, bf16[4,32,8,128]{3,2,1,0:T(8,128)(2,1)}, u32[]{:S(2)}, u32[]{:S(2)}) collective-permute-start(bf16[4,32,8,128]{3,2,1,0:T(8,128)(2,1)S(1)} %bitcast.43), channel_id=1, source_target_pairs={{0,32},{32,0},{64,96},{96,64},{128,160},{160,128},{192,224},{224,1... | collective-permute-start | bytes 786440 | tf_op jit(solution)/shard_map/ppermute | solution.py:301

commit v4 on v3

--- a/solution.py
+++ b/solution.py
@@ -143,7 +143,7 @@
 def decode_kernel(
     first, rest, out_g, out_u, scale_g, scale_u, pick, sums, ready, sems, scales, scale_sems, *pairs
 ):
-    spreads, values, factors = pairs[0:2], pairs[2:4], pairs[4:6]
+    spreads, values, totals = pairs[0:2], pairs[2:4], pairs[4:6]
     parts = first.shape[0]
     width = first.shape[1] - 8
     rows = width * PAIR
@@ -161,10 +161,10 @@
     wanted = 32 * (tile % tiles) + 2 * (tile // tiles) + at // half
     pick[...] = (source == wanted).astype(jnp.bfloat16)
 
-    def copies(step, slot):
+    def copies(step):
         where = pl.ds(pl.multiple_of(step * rows, rows), rows)
         return [
-            pltpu.make_async_copy(ready.at[slot, m], out.at[where, :], sems.at[slot, m])
+            pltpu.make_async_copy(ready.at[step, m], out.at[where, :], sems.at[step, m])
             for m, out in enumerate((out_g, out_u))
         ]
 
@@ -183,35 +183,34 @@
                 c = whole[8 * k : 8 * k + 8]
                 scale = spreads[side][src * 8 : src * 8 + 8, k * LANES : (k + 1) * LANES]
                 size = jnp.log2(jnp.maximum(jnp.abs(c), SMALLEST))
-                value = (c * scale) * jnp.exp2(size * (1.0 / POWER - 1.0))
+                value = (c * jnp.exp2(size * (1.0 / POWER - 1.0))) * scale
                 acc[k] = acc[k] + jnp.abs(value)
                 values[side][src, 8 * k : 8 * k + 8, :] = value
         for k in range(PAIR * tiles):
+            totals[side][8 * k : 8 * k + 8, :] = acc[k]
+
+    def write(step, side):
+        factor = []
+        for k in range(PAIR * tiles):
             at = slice(8 * k, 8 * k + 8)
-            sg = jnp.sum(jnp.where(left, acc[k], 0.0), axis=1, keepdims=True) * (1.0 / total)
-            su = jnp.sum(jnp.where(left, 0.0, acc[k]), axis=1, keepdims=True) * (1.0 / total)
+            acc = totals[side][at, :]
+            sg = jnp.sum(jnp.where(left, acc, 0.0), axis=1, keepdims=True) * (1.0 / total)
+            su = jnp.sum(jnp.where(left, 0.0, acc), axis=1, keepdims=True) * (1.0 / total)
             sums[at, :] += jnp.where(
                 lane == 2 * step, sg, jnp.where(lane == 2 * step + 1, su, 0.0)
             )
-            factors[side][at, :] = 1.0 / jnp.where(left, sg, su)
-
-    def write(step, side):
+            factor.append(1.0 / jnp.where(left, sg, su))
         for t in range(parts // 2):
             for k in range(PAIR * tiles):
                 at = slice(8 * k, 8 * k + 8)
-                factor = factors[side][at, :]
-                even = values[side][2 * t, at, :] * factor
-                odd = values[side][2 * t + 1, at, :] * factor
+                even = values[side][2 * t, at, :] * factor[k]
+                odd = values[side][2 * t + 1, at, :] * factor[k]
                 g = jnp.where(left, even, pltpu.roll(odd, half, 1))
                 u = jnp.where(left, pltpu.roll(even, half, 1), odd)
                 for m, whole in enumerate((g, u)):
-                    ready[side, m, at, t * LANES : (t + 1) * LANES] = whole.astype(jnp.bfloat16)
-        for copy in copies(step, side):
+                    ready[step, m, at, t * LANES : (t + 1) * LANES] = whole.astype(jnp.bfloat16)
+        for copy in copies(step):
             copy.start()
-
-    def wait(step, side):
-        for copy in copies(step, side):
-            copy.wait()
 
     def from_rest(step, side):
         start = pl.multiple_of(step * rows - width, 8)
@@ -229,19 +228,14 @@
     def _(i):
         for side in (1, 0):
             step = 2 * i + 2 - side
-
-            @pl.when(i > 0)
-            def _():
-                wait(step - 3, 1 - side)
-
             write(step - 1, 1 - side)
             spread_norms(step + 1, 1 - side)
             from_rest(step, side)
 
     last = steps - 1
-    wait(last - 3, 0)
     write(last - 1, 0)
     from_rest(jnp.int32(last), 1)
+    write(last, 1)
     turned = jnp.concatenate(
         [sums[...], jnp.zeros((LANES - rows, LANES), jnp.float32)], axis=0
     ).T
@@ -252,12 +246,13 @@
             scales[m, pl.ds(p, steps, stride=PAIR), :] = turned[:, m, p * width : (p + 1) * width]
         scale_copies.append(pltpu.make_async_copy(scales.at[m], out, scale_sems.at[m]))
         scale_copies[m].start()
-    wait(last - 2, 1)
-    write(last, 1)
-    wait(last - 1, 0)
-    wait(last, 1)
     for copy in scale_copies:
         copy.wait()
+
+    @pl.loop(0, steps)
+    def _(step):
+        for copy in copies(step):
+            copy.wait()
 
 
 def decode(experts, first, rest):
@@ -265,6 +260,7 @@
     width = rows - 8
     rows = width * PAIR
     total = parts * lanes // 2
+    steps = experts // PAIR
     ready = jax.ShapeDtypeStruct((experts * width, total), jnp.bfloat16)
     scale = jax.ShapeDtypeStruct((experts, width), jnp.float32)
     vmem, anywhere = pl.BlockSpec(memory_space=pltpu.VMEM), pl.BlockSpec(memory_space=pl.ANY)
@@ -276,8 +272,8 @@
         scratch_shapes=[
             pltpu.VMEM((lanes, rows // 8 * lanes), jnp.bfloat16),
             pltpu.VMEM((rows, lanes), jnp.float32),
-            pltpu.VMEM((2, 2, rows, total), jnp.bfloat16),
-            pltpu.SemaphoreType.DMA((2, 2)),
+            pltpu.VMEM((steps, 2, rows, total), jnp.bfloat16),
+            pltpu.SemaphoreType.DMA((steps, 2)),
             pltpu.VMEM((2, experts, width), jnp.float32),
             pltpu.SemaphoreType.DMA((2,)),
             *[pltpu.VMEM((parts * 8, rows // 8 * lanes), jnp.float32)] * 2,

time: 107 us -> 107 us (level)
  no operation moved by 1% of the time
where the time goes in v4:
time: 107 us; the launch traced here: 105 us
  waiting for transfers between devices  56.9 us (53%)
  starting transfers between devices  19.9 us (19%)
  Pallas kernels  14.4 us (13%)
  local copies, waits for them, and re-layouts  11.2 us (10%)
  other arithmetic  1.77 us (2%)
    all_to_all x2, waiting for transfers between devices, per_device(): lax.all_to_all(a, 'fsdp', split_axis=0, concat_axis=0, tiled=True)  46.5 us
    all_to_all x2, starting transfers between devices, per_device(): lax.all_to_all(a, 'fsdp', split_axis=0, concat_axis=0, tiled=True)  17.5 us
    ppermute x3, waiting for transfers between devices, gathered(): other = lax.ppermute(held, axis, [(i, i ^ bit) for i in range(n)])  10.4 us
    pallas_call x1, Pallas kernels, encode_rest(): pl.pallas_call(kernel, in_specs=[anywhere] * 4 + [vmem], out_specs=anywhe...  7.3 us
    pallas_call x1, Pallas kernels, decode(): pl.pallas_call(decode_kernel, in_specs=[vmem, vmem], out_specs=[anywhere]...  5.05 us
    another operation x1, local copies, waits for them, and re-layouts, per_device(): router = router.reshape(groups, parts, 8, 2, half).transpose(1, 4, 0, 3, 2)  3.17 us
    reshape x1, local copies, waits for them, and re-layouts, per_device(): serve_router = router.reshape(parts * half, groups * 16)  2.71 us
    transpose x1, local copies, waits for them, and re-layouts, per_device(): router = router.reshape(groups, parts, 8, 2, half).transpose(1, 4, 0, 3, 2)  2.47 us
  transfers between devices with their start and end apart: 5, of which 5 were waited for; matrix products, arithmetic and copies ran while one was open for 12% of the time, Pallas kernels for 7%

profile of v4, /device:TPU:22, one launch (start us, length us, event | category | flops | bytes accessed | tf_op | source)
XLA Modules:
  0.0 105.0 jit_solution(2235299158896995197)
XLA Ops:
  0.6 2.1 %encode_first.1 = (bf16[32,32,128]{2,1,0:T(8,128)(2,1)}, f32[8,768]{1,0:T(8,128)}) custom-call(f32[16,64,768]{2,1,0:T(8,128)} %tg.3, bf16[16,64,768]{2,1,0:T(8,128)(2,1)} %og.3, f32[16,64,768]{2,1,0:T(8,128)} %tu.3, bf16[16,64,768]{2,1,0:T(8,128)(2,1)} %ou.3, f32[16,64]{1,0:T(8,128)} %bitcast.44, f32[1,64]{1,0:T(1,128)} %bitcast.45), custom_call_target="tpu_custom_call" | custom-call | flops 25000000 | bytes 900000 | tf_op jit(solution)/shard_map/encode_first/pallas_call | solution.py:55
  2.7 11.6 %all-to-all-start = ((bf16[32,32,128]{2,1,0:T(8,128)(2,1)}), bf16[32,32,128]{2,1,0:T(8,128)(2,1)S(1)}, u32[]{:S(2)}, u32[]{:S(2)}) async-start(bf16[32,32,128]{2,1,0:T(8,128)(2,1)} %get-tuple-element.11), calls=%async_computation | async-start | bytes 524288 | tf_op jit(solution)/shard_map/all_to_all | solution.py:309
  14.3 7.3 %encode_rest.1 = bf16[32,368,128]{2,1,0:T(8,128)(2,1)} custom-call(f32[16,64,768]{2,1,0:T(8,128)} %tg.3, bf16[16,64,768]{2,1,0:T(8,128)(2,1)} %og.3, f32[16,64,768]{2,1,0:T(8,128)} %tu.3, bf16[16,64,768]{2,1,0:T(8,128)(2,1)} %ou.3, f32[8,768]{1,0:T(8,128)} %get-tuple-element.12.before), custom_call_target="tpu_custom_call" | custom-call | flops 400000000 | bytes 11000000 | tf_op jit(solution)/shard_map/encode_rest/pallas_call | solution.py:124
  21.6 3.9 %all-to-all-done.first = bf16[32,32,128]{2,1,0:T(8,128)(2,1)S(1)} async-done(((bf16[32,32,128]{2,1,0:T(8,128)(2,1)}), bf16[32,32,128]{2,1,0:T(8,128)(2,1)S(1)}, u32[]{:S(2)}, u32[]{:S(2)}) %all-to-all-start) | async-done | bytes 262176 | tf_op jit(solution)/shard_map/all_to_all | solution.py:309
  25.5 5.9 %all-to-all-start.1 = ((bf16[32,368,128]{2,1,0:T(8,128)(2,1)}), bf16[32,368,128]{2,1,0:T(8,128)(2,1)S(1)}, u32[]{:S(2)}, u32[]{:S(2)}) async-start(bf16[32,368,128]{2,1,0:T(8,128)(2,1)} %encode_rest.1), calls=%async_computation.1 | async-start | bytes 6029312 | tf_op jit(solution)/shard_map/all_to_all | solution.py:309
  31.4 1.5 %collective-permute-start = (bf16[1,32,8,128]{3,2,1,0:T(8,128)(2,1)S(1)}, bf16[1,32,8,128]{3,2,1,0:T(8,128)(2,1)S(1)}, u32[]{:S(2)}, u32[]{:S(2)}) collective-permute-start(bf16[1,32,8,128]{3,2,1,0:T(8,128)(2,1)S(1)} %slice_bitcast_fusion), channel_id=1, source_target_pairs={{0,128},{32,160},{64,192},{96,224},{128,0},{160,32},{192,64},{224,... | collective-permute-start | bytes 196616 | tf_op jit(solution)/shard_map/ppermute | solution.py:297
  32.9 4.4 %collective-permute-done = bf16[1,32,8,128]{3,2,1,0:T(8,128)(2,1)S(1)} collective-permute-done((bf16[1,32,8,128]{3,2,1,0:T(8,128)(2,1)S(1)}, bf16[1,32,8,128]{3,2,1,0:T(8,128)(2,1)S(1)}, u32[]{:S(2)}, u32[]{:S(2)}) %collective-permute-start) | collective-permute-done | bytes 65568 | tf_op jit(solution)/shard_map/ppermute | solution.py:297
  37.3 0.7 maximum_bitcast_fusion
  38.0 0.8 collective-permute-start.1
  38.8 4.3 %collective-permute-done.1 = bf16[2,32,8,128]{3,2,1,0:T(8,128)(2,1)S(1)} collective-permute-done((bf16[2,32,8,128]{3,2,1,0:T(8,128)(2,1)}, bf16[2,32,8,128]{3,2,1,0:T(8,128)(2,1)S(1)}, u32[]{:S(2)}, u32[]{:S(2)}) %collective-permute-start.1) | collective-permute-done | bytes 131104 | tf_op jit(solution)/shard_map/ppermute | solution.py:297
  43.2 0.1 collective-permute-start.2
  43.3 1.6 %collective-permute-done.2 = bf16[4,32,8,128]{3,2,1,0:T(8,128)(2,1)} collective-permute-done((bf16[4,32,8,128]{3,2,1,0:T(8,128)(2,1)S(1)}, bf16[4,32,8,128]{3,2,1,0:T(8,128)(2,1)}, u32[]{:S(2)}, u32[]{:S(2)}) %collective-permute-start.2) | collective-permute-done | bytes 262176 | tf_op jit(solution)/shard_map/ppermute | solution.py:297
  45.0 1.0 select_bitcast_fusion.1
  46.0 0.1 pad_maximum_fusion
  46.1 0.8 copy.12
  46.9 3.2 %reshape_reshape.3 = bf16[8,32,8,2,64]{4,3,2,1,0:T(2,128)(2,1)} reshape(bf16[4,2,32,8,128]{4,3,2,1,0:T(8,128)(2,1)} %copy.12) | data formatting | bytes 1048576 | tf_op jit(solution)/shard_map/reshape;reshape | solution.py:317
  50.1 2.5 %copy.13 = bf16[32,64,8,2,8]{1,0,4,3,2:T(8,128)(2,1)} copy(bf16[32,64,8,2,8]{1,3,4,0,2:T(2,128)(2,1)} %bitcast.42) | data formatting | bytes 1048576 | tf_op jit(solution)/shard_map/transpose | solution.py:317
  52.5 2.7 %reshape.29 = bf16[2048,128]{0,1:T(8,128)(2,1)} reshape(bf16[32,64,8,2,8]{1,0,4,3,2:T(8,128)(2,1)} %copy.13) | data formatting | bytes 1048576 | tf_op jit(solution)/shard_map/reshape | solution.py:318
  55.2 2.0 %copy.14 = bf16[2048,128]{1,0:T(8,128)(2,1)} copy(bf16[2048,128]{0,1:T(8,128)(2,1)} %reshape.29) | data formatting | bytes 1048576
  57.3 42.6 %all-to-all-done.1.rest = bf16[32,368,128]{2,1,0:T(8,128)(2,1)S(1)} async-done(((bf16[32,368,128]{2,1,0:T(8,128)(2,1)}), bf16[32,368,128]{2,1,0:T(8,128)(2,1)S(1)}, u32[]{:S(2)}, u32[]{:S(2)}) %all-to-all-start.1) | async-done | bytes 3014688 | tf_op jit(solution)/shard_map/all_to_all | solution.py:309
  99.9 5.0 %decode.1 = (bf16[384,2048]{1,0:T(8,128)(2,1)}, bf16[384,2048]{1,0:T(8,128)(2,1)}, f32[16,24]{1,0:T(8,128)}, f32[16,24]{1,0:T(8,128)}) custom-call(bf16[32,32,128]{2,1,0:T(8,128)(2,1)S(1)} %all-to-all-done.first, bf16[32,368,128]{2,1,0:T(8,128)(2,1)S(1)} %all-to-all-done.1.rest), custom_call_target="tpu_custom_call" | custom-call | flops 400000000 | bytes 6400000 | tf_op jit(solution)/shard_map/decode/pallas_call | solution.py:267
  (5 shorter events, 0.1 us)
Async XLA Ops:
  2.7 22.8 %all-to-all-start = ((bf16[32,32,128]{2,1,0:T(8,128)(2,1)}), bf16[32,32,128]{2,1,0:T(8,128)(2,1)S(1)}, u32[]{:S(2)}, u32[]{:S(2)}) async-start(bf16[32,32,128]{2,1,0:T(8,128)(2,1)} %get-tuple-element.11), calls=%async_computation | async-start | bytes 524288 | tf_op jit(solution)/shard_map/all_to_all | solution.py:309
  25.5 74.4 %all-to-all-start.1 = ((bf16[32,368,128]{2,1,0:T(8,128)(2,1)}), bf16[32,368,128]{2,1,0:T(8,128)(2,1)S(1)}, u32[]{:S(2)}, u32[]{:S(2)}) async-start(bf16[32,368,128]{2,1,0:T(8,128)(2,1)} %encode_rest.1), calls=%async_computation.1 | async-start | bytes 6029312 | tf_op jit(solution)/shard_map/all_to_all | solution.py:309
  31.4 5.9 %collective-permute-start = (bf16[1,32,8,128]{3,2,1,0:T(8,128)(2,1)S(1)}, bf16[1,32,8,128]{3,2,1,0:T(8,128)(2,1)S(1)}, u32[]{:S(2)}, u32[]{:S(2)}) collective-permute-start(bf16[1,32,8,128]{3,2,1,0:T(8,128)(2,1)S(1)} %slice_bitcast_fusion), channel_id=1, source_target_pairs={{0,128},{32,160},{64,192},{96,224},{128,0},{160,32},{192,64},{224,... | collective-permute-start | bytes 196616 | tf_op jit(solution)/shard_map/ppermute | solution.py:297
  38.0 5.2 %collective-permute-start.1 = (bf16[2,32,8,128]{3,2,1,0:T(8,128)(2,1)}, bf16[2,32,8,128]{3,2,1,0:T(8,128)(2,1)S(1)}, u32[]{:S(2)}, u32[]{:S(2)}) collective-permute-start(bf16[2,32,8,128]{3,2,1,0:T(8,128)(2,1)} %maximum_bitcast_fusion), channel_id=1, source_target_pairs={{0,64},{32,96},{64,0},{96,32},{128,192},{160,224},{192,128},{224,1... | collective-permute-start | bytes 393224 | tf_op jit(solution)/shard_map/ppermute | solution.py:297
  43.2 1.8 %collective-permute-start.2 = (bf16[4,32,8,128]{3,2,1,0:T(8,128)(2,1)S(1)}, bf16[4,32,8,128]{3,2,1,0:T(8,128)(2,1)}, u32[]{:S(2)}, u32[]{:S(2)}) collective-permute-start(bf16[4,32,8,128]{3,2,1,0:T(8,128)(2,1)S(1)} %bitcast.43), channel_id=1, source_target_pairs={{0,32},{32,0},{64,96},{96,64},{128,160},{160,128},{192,224},{224,1... | collective-permute-start | bytes 786440 | tf_op jit(solution)/shard_map/ppermute | solution.py:297

commit v5 on v4

--- a/solution.py
+++ b/solution.py
@@ -26,10 +26,15 @@
     return (v8 * v4) * (v2 * v), norm
 
 
+def backwards(blocks):
+    return jnp.concatenate([blocks[k : k + 1] for k in reversed(range(len(blocks)))], axis=0)
+
+
 def coded_expert(parts, tg, og, tu, ou):
     cg, ng = coded(tg[...] + og[...].astype(jnp.float32))
     cu, nu = coded(tu[...] + ou[...].astype(jnp.float32))
-    return jnp.concatenate([cg, cu], axis=0).T.reshape(parts, -1, LANES), ng, nu
+    codes = jnp.concatenate([cg, cu], axis=0).T.reshape(parts, -1, LANES)
+    return backwards(codes), ng, nu
 
 
 def first_kernel(parts, tg, og, tu, ou, weight, gain, out, norms):
@@ -101,7 +106,7 @@
     packed = turned[:, 0]
     for k in range(1, width // 8):
         packed = packed + pltpu.roll(turned[:, k], 32 * k, 2)
-    norm_rows[...] = packed.astype(jnp.bfloat16)
+    norm_rows[...] = backwards(packed).astype(jnp.bfloat16)
     last = pltpu.make_async_copy(norm_rows, out.at[:, pl.ds(count * width, 8), :], norm_sem)
     last.start()
 
@@ -178,10 +183,11 @@
     def read(step, side, codes_of):
         acc = [jnp.zeros((8, LANES), jnp.float32) for _ in range(PAIR * tiles)]
         for src in range(parts):
-            whole = codes_of(src).astype(jnp.float32)
+            block = parts - 1 - src
+            whole = codes_of(block).astype(jnp.float32)
             for k in range(PAIR * tiles):
                 c = whole[8 * k : 8 * k + 8]
-                scale = spreads[side][src * 8 : src * 8 + 8, k * LANES : (k + 1) * LANES]
+                scale = spreads[side][block * 8 : block * 8 + 8, k * LANES : (k + 1) * LANES]
                 size = jnp.log2(jnp.maximum(jnp.abs(c), SMALLEST))
                 value = (c * jnp.exp2(size * (1.0 / POWER - 1.0))) * scale
                 acc[k] = acc[k] + jnp.abs(value)
@@ -214,14 +220,14 @@
 
     def from_rest(step, side):
         start = pl.multiple_of(step * rows - width, 8)
-        read(step, side, lambda src: rest[src, pl.ds(start, rows), :])
+        read(step, side, lambda block: rest[block, pl.ds(start, rows), :])
 
     spread_norms(jnp.int32(0), 0)
     spread_norms(jnp.int32(1), 1)
     read(
         jnp.int32(0),
         0,
-        lambda src: jnp.concatenate([first[src, :width, :], rest[src, :width, :]], axis=0),
+        lambda block: jnp.concatenate([first[block, :width, :], rest[block, :width, :]], axis=0),
     )
 
     @pl.loop(0, steps // 2 - 1)
@@ -306,13 +312,16 @@
     experts = train_gate.shape[0]
     parts = lax.axis_size("fsdp")
     latest = (train_gate, other_gate, train_up, other_up)
-    sent = lambda a: lax.all_to_all(a, "fsdp", split_axis=0, concat_axis=0, tiled=True)
+    order = [list(range(parts))[::-1]]
+    sent = lambda a: lax.all_to_all(
+        a, "fsdp", split_axis=0, concat_axis=0, axis_index_groups=order, tiled=True
+    )
 
     codes, norms = encode_first(parts, *latest, router_weight.T, router_gain[None])
     first = sent(codes)
     rest = sent(encode_rest(parts, *latest, norms))
 
-    router = gathered(first[:, -8:, :], "ep")
+    router = gathered(first[::-1, -8:, :], "ep")
     groups, half = router.shape[0], LANES // 2
     router = router.reshape(groups, parts, 8, 2, half).transpose(1, 4, 0, 3, 2)
     serve_router = router.reshape(parts * half, groups * 16)

time: 107 us -> 104 us (0.972)
  waiting for transfers between devices: 56.9 us -> 52.1 us
    all_to_all x2, waiting for transfers between devices: 46.5 us -> 41.6 us  [per_device(): lax.all_to_all(a, 'fsdp', split_axis=0, concat_axis=0, axis_index_groups=...]
  transfers between devices with their start and end apart: 5 -> 5, of which waited for: 5 -> 5; matrix products, arithmetic and copies ran while one was open for 12% -> 14% of each run, Pallas kernels for 7% -> 7%
where the time goes in v5:
time: 104 us; the launch traced here: 102 us
  waiting for transfers between devices  52.1 us (50%)
  starting transfers between devices  20.8 us (20%)
  Pallas kernels  14.5 us (14%)
  local copies, waits for them, and re-layouts  11.3 us (11%)
  other arithmetic  2.69 us (3%)
    all_to_all x2, waiting for transfers between devices, per_device(): lax.all_to_all(a, 'fsdp', split_axis=0, concat_axis=0, axis_index_groups=...  41.6 us
    all_to_all x2, starting transfers between devices, per_device(): lax.all_to_all(a, 'fsdp', split_axis=0, concat_axis=0, axis_index_groups=...  18.4 us
    ppermute x3, waiting for transfers between devices, gathered(): other = lax.ppermute(held, axis, [(i, i ^ bit) for i in range(n)])  10.5 us
    pallas_call x1, Pallas kernels, encode_rest(): pl.pallas_call(kernel, in_specs=[anywhere] * 4 + [vmem], out_specs=anywhe...  7.3 us
    pallas_call x1, Pallas kernels, decode(): pl.pallas_call(decode_kernel, in_specs=[vmem, vmem], out_specs=[anywhere]...  5.17 us
    another operation x1, local copies, waits for them, and re-layouts, per_device(): router = router.reshape(groups, parts, 8, 2, half).transpose(1, 4, 0, 3, 2)  3.17 us
    reshape x1, local copies, waits for them, and re-layouts, per_device(): serve_router = router.reshape(parts * half, groups * 16)  2.71 us
    transpose x1, local copies, waits for them, and re-layouts, per_device(): router = router.reshape(groups, parts, 8, 2, half).transpose(1, 4, 0, 3, 2)  2.47 us
  transfers between devices with their start and end apart: 5, of which 5 were waited for; matrix products, arithmetic and copies ran while one was open for 14% of the time, Pallas kernels for 7%

profile of v5, /device:TPU:22, one launch (start us, length us, event | category | flops | bytes accessed | tf_op | source)
XLA Modules:
  0.0 102.1 jit_solution(7117819032875802327)
XLA Ops:
  0.6 2.1 %encode_first.1 = (bf16[32,32,128]{2,1,0:T(8,128)(2,1)}, f32[8,768]{1,0:T(8,128)}) custom-call(f32[16,64,768]{2,1,0:T(8,128)} %tg.3, bf16[16,64,768]{2,1,0:T(8,128)(2,1)} %og.3, f32[16,64,768]{2,1,0:T(8,128)} %tu.3, bf16[16,64,768]{2,1,0:T(8,128)(2,1)} %ou.3, f32[16,64]{1,0:T(8,128)} %bitcast.44, f32[1,64]{1,0:T(1,128)} %bitcast.45), custom_call_target="tpu_custom_call" | custom-call | flops 25000000 | bytes 900000 | tf_op jit(solution)/shard_map/encode_first/pallas_call | solution.py:60
  2.7 10.7 %all-to-all-start = ((bf16[32,32,128]{2,1,0:T(8,128)(2,1)}), bf16[32,32,128]{2,1,0:T(8,128)(2,1)S(1)}, u32[]{:S(2)}, u32[]{:S(2)}) async-start(bf16[32,32,128]{2,1,0:T(8,128)(2,1)} %get-tuple-element.11), calls=%async_computation | async-start | bytes 524288 | tf_op jit(solution)/shard_map/all_to_all | solution.py:316
  13.4 7.3 %encode_rest.1 = bf16[32,368,128]{2,1,0:T(8,128)(2,1)} custom-call(f32[16,64,768]{2,1,0:T(8,128)} %tg.3, bf16[16,64,768]{2,1,0:T(8,128)(2,1)} %og.3, f32[16,64,768]{2,1,0:T(8,128)} %tu.3, bf16[16,64,768]{2,1,0:T(8,128)(2,1)} %ou.3, f32[8,768]{1,0:T(8,128)} %get-tuple-element.12.before), custom_call_target="tpu_custom_call" | custom-call | flops 400000000 | bytes 11000000 | tf_op jit(solution)/shard_map/encode_rest/pallas_call | solution.py:129
  20.7 2.1 %all-to-all-done.first = bf16[32,32,128]{2,1,0:T(8,128)(2,1)S(1)} async-done(((bf16[32,32,128]{2,1,0:T(8,128)(2,1)}), bf16[32,32,128]{2,1,0:T(8,128)(2,1)S(1)}, u32[]{:S(2)}, u32[]{:S(2)}) %all-to-all-start) | async-done | bytes 262176 | tf_op jit(solution)/shard_map/all_to_all | solution.py:316
  22.8 7.7 %all-to-all-start.1 = ((bf16[32,368,128]{2,1,0:T(8,128)(2,1)}), bf16[32,368,128]{2,1,0:T(8,128)(2,1)S(1)}, u32[]{:S(2)}, u32[]{:S(2)}) async-start(bf16[32,368,128]{2,1,0:T(8,128)(2,1)} %encode_rest.1), calls=%async_computation.1 | async-start | bytes 6029312 | tf_op jit(solution)/shard_map/all_to_all | solution.py:316
  30.5 1.5 %collective-permute-start = (bf16[1,32,8,128]{3,2,1,0:T(8,128)(2,1)S(1)}, bf16[1,32,8,128]{3,2,1,0:T(8,128)(2,1)S(1)}, u32[]{:S(2)}, u32[]{:S(2)}) collective-permute-start(bf16[1,32,8,128]{3,2,1,0:T(8,128)(2,1)S(1)} %reverse_bitcast_fusion), channel_id=1, source_target_pairs={{0,128},{32,160},{64,192},{96,224},{128,0},{160,32},{192,64},{224,... | collective-permute-start | bytes 196616 | tf_op jit(solution)/shard_map/ppermute | solution.py:303
  32.0 4.4 %collective-permute-done = bf16[1,32,8,128]{3,2,1,0:T(8,128)(2,1)S(1)} collective-permute-done((bf16[1,32,8,128]{3,2,1,0:T(8,128)(2,1)S(1)}, bf16[1,32,8,128]{3,2,1,0:T(8,128)(2,1)S(1)}, u32[]{:S(2)}, u32[]{:S(2)}) %collective-permute-start) | collective-permute-done | bytes 65568 | tf_op jit(solution)/shard_map/ppermute | solution.py:303
  36.4 0.7 maximum_bitcast_fusion
  37.1 0.8 collective-permute-start.1
  37.9 4.5 %collective-permute-done.1 = bf16[2,32,8,128]{3,2,1,0:T(8,128)(2,1)} collective-permute-done((bf16[2,32,8,128]{3,2,1,0:T(8,128)(2,1)}, bf16[2,32,8,128]{3,2,1,0:T(8,128)(2,1)}, u32[]{:S(2)}, u32[]{:S(2)}) %collective-permute-start.1) | collective-permute-done | bytes 131104 | tf_op jit(solution)/shard_map/ppermute | solution.py:303
  42.4 0.9 select_bitcast_fusion.3
  43.3 0.1 collective-permute-start.2
  43.5 1.6 %collective-permute-done.2 = bf16[4,32,8,128]{3,2,1,0:T(8,128)(2,1)} collective-permute-done((bf16[4,32,8,128]{3,2,1,0:T(8,128)(2,1)S(1)}, bf16[4,32,8,128]{3,2,1,0:T(8,128)(2,1)}, u32[]{:S(2)}, u32[]{:S(2)}) %collective-permute-start.2) | collective-permute-done | bytes 262176 | tf_op jit(solution)/shard_map/ppermute | solution.py:303
  45.1 1.0 select_bitcast_fusion.1
  46.1 0.1 pad_maximum_fusion
  46.2 0.8 copy.12
  47.0 3.2 %reshape_reshape.3 = bf16[8,32,8,2,64]{4,3,2,1,0:T(2,128)(2,1)} reshape(bf16[4,2,32,8,128]{4,3,2,1,0:T(8,128)(2,1)} %copy.12) | data formatting | bytes 1048576 | tf_op jit(solution)/shard_map/reshape;reshape | solution.py:326
  50.2 2.5 %copy.13 = bf16[32,64,8,2,8]{1,0,4,3,2:T(8,128)(2,1)} copy(bf16[32,64,8,2,8]{1,3,4,0,2:T(2,128)(2,1)} %bitcast.42) | data formatting | bytes 1048576 | tf_op jit(solution)/shard_map/transpose | solution.py:326
  52.6 2.7 %reshape.29 = bf16[2048,128]{0,1:T(8,128)(2,1)} reshape(bf16[32,64,8,2,8]{1,0,4,3,2:T(8,128)(2,1)} %copy.13) | data formatting | bytes 1048576 | tf_op jit(solution)/shard_map/reshape | solution.py:327
  55.3 2.0 %copy.14 = bf16[2048,128]{1,0:T(8,128)(2,1)} copy(bf16[2048,128]{0,1:T(8,128)(2,1)} %reshape.29) | data formatting | bytes 1048576
  57.4 39.6 %all-to-all-done.1.rest = bf16[32,368,128]{2,1,0:T(8,128)(2,1)S(1)} async-done(((bf16[32,368,128]{2,1,0:T(8,128)(2,1)}), bf16[32,368,128]{2,1,0:T(8,128)(2,1)S(1)}, u32[]{:S(2)}, u32[]{:S(2)}) %all-to-all-start.1) | async-done | bytes 3014688 | tf_op jit(solution)/shard_map/all_to_all | solution.py:316
  96.9 5.2 %decode.1 = (bf16[384,2048]{1,0:T(8,128)(2,1)}, bf16[384,2048]{1,0:T(8,128)(2,1)}, f32[16,24]{1,0:T(8,128)}, f32[16,24]{1,0:T(8,128)}) custom-call(bf16[32,32,128]{2,1,0:T(8,128)(2,1)S(1)} %all-to-all-done.first, bf16[32,368,128]{2,1,0:T(8,128)(2,1)S(1)} %all-to-all-done.1.rest), custom_call_target="tpu_custom_call" | custom-call | flops 400000000 | bytes 6400000 | tf_op jit(solution)/shard_map/decode/pallas_call | solution.py:273
  (5 shorter events, 0.1 us)
Async XLA Ops:
  2.7 20.0 %all-to-all-start = ((bf16[32,32,128]{2,1,0:T(8,128)(2,1)}), bf16[32,32,128]{2,1,0:T(8,128)(2,1)S(1)}, u32[]{:S(2)}, u32[]{:S(2)}) async-start(bf16[32,32,128]{2,1,0:T(8,128)(2,1)} %get-tuple-element.11), calls=%async_computation | async-start | bytes 524288 | tf_op jit(solution)/shard_map/all_to_all | solution.py:316
  22.8 74.2 %all-to-all-start.1 = ((bf16[32,368,128]{2,1,0:T(8,128)(2,1)}), bf16[32,368,128]{2,1,0:T(8,128)(2,1)S(1)}, u32[]{:S(2)}, u32[]{:S(2)}) async-start(bf16[32,368,128]{2,1,0:T(8,128)(2,1)} %encode_rest.1), calls=%async_computation.1 | async-start | bytes 6029312 | tf_op jit(solution)/shard_map/all_to_all | solution.py:316
  30.5 5.9 %collective-permute-start = (bf16[1,32,8,128]{3,2,1,0:T(8,128)(2,1)S(1)}, bf16[1,32,8,128]{3,2,1,0:T(8,128)(2,1)S(1)}, u32[]{:S(2)}, u32[]{:S(2)}) collective-permute-start(bf16[1,32,8,128]{3,2,1,0:T(8,128)(2,1)S(1)} %reverse_bitcast_fusion), channel_id=1, source_target_pairs={{0,128},{32,160},{64,192},{96,224},{128,0},{160,32},{192,64},{224,... | collective-permute-start | bytes 196616 | tf_op jit(solution)/shard_map/ppermute | solution.py:303
  37.1 5.3 %collective-permute-start.1 = (bf16[2,32,8,128]{3,2,1,0:T(8,128)(2,1)}, bf16[2,32,8,128]{3,2,1,0:T(8,128)(2,1)}, u32[]{:S(2)}, u32[]{:S(2)}) collective-permute-start(bf16[2,32,8,128]{3,2,1,0:T(8,128)(2,1)} %maximum_bitcast_fusion), channel_id=1, source_target_pairs={{0,64},{32,96},{64,0},{96,32},{128,192},{160,224},{192,128},{224,1... | collective-permute-start | bytes 393224 | tf_op jit(solution)/shard_map/ppermute | solution.py:303
  43.3 1.8 %collective-permute-start.2 = (bf16[4,32,8,128]{3,2,1,0:T(8,128)(2,1)S(1)}, bf16[4,32,8,128]{3,2,1,0:T(8,128)(2,1)}, u32[]{:S(2)}, u32[]{:S(2)}) collective-permute-start(bf16[4,32,8,128]{3,2,1,0:T(8,128)(2,1)S(1)} %bitcast.43), channel_id=1, source_target_pairs={{0,32},{32,0},{64,96},{96,64},{128,160},{160,128},{192,224},{224,1... | collective-permute-start | bytes 786440 | tf_op jit(solution)/shard_map/ppermute | solution.py:303

commit v6 on v5

--- a/solution.py
+++ b/solution.py
@@ -26,6 +26,10 @@
     return (v8 * v4) * (v2 * v), norm
 
 
+def swapped(blocks, at=4):
+    return [*blocks[at : 2 * at], *blocks[:at], *blocks[2 * at :]]
+
+
 def backwards(blocks):
     return jnp.concatenate([blocks[k : k + 1] for k in reversed(range(len(blocks)))], axis=0)
 
@@ -46,6 +50,7 @@
     codes, norms[0:1, :], norms[1:2, :] = coded_expert(
         parts, *(a.at[0] for a in (tg, og, tu, ou))
     )
+    codes = jnp.concatenate([codes[b : b + 1] for b in swapped(range(parts))], axis=0)
     for k in range(0, width, 8):
         out[:, k : k + 8, :] = codes[:, k : k + 8].astype(jnp.bfloat16)
 
@@ -227,7 +232,9 @@
     read(
         jnp.int32(0),
         0,
-        lambda block: jnp.concatenate([first[block, :width, :], rest[block, :width, :]], axis=0),
+        lambda block: jnp.concatenate(
+            [first[swapped(range(parts))[block], :width, :], rest[block, :width, :]], axis=0
+        ),
     )
 
     @pl.loop(0, steps // 2 - 1)
@@ -312,16 +319,18 @@
     experts = train_gate.shape[0]
     parts = lax.axis_size("fsdp")
     latest = (train_gate, other_gate, train_up, other_up)
-    order = [list(range(parts))[::-1]]
-    sent = lambda a: lax.all_to_all(
-        a, "fsdp", split_axis=0, concat_axis=0, axis_index_groups=order, tiled=True
+    order = list(range(parts))[::-1]
+    sent = lambda a, order: lax.all_to_all(
+        a, "fsdp", split_axis=0, concat_axis=0, axis_index_groups=[order], tiled=True
     )
 
     codes, norms = encode_first(parts, *latest, router_weight.T, router_gain[None])
-    first = sent(codes)
-    rest = sent(encode_rest(parts, *latest, norms))
-
-    router = gathered(first[::-1, -8:, :], "ep")
+    first = sent(codes, swapped(order))
+    rest = sent(encode_rest(parts, *latest, norms), order)
+
+    router = first[:, -8:, :]
+    router = jnp.concatenate([router[4:8], router[:4], router[8:]], axis=0)
+    router = gathered(router[::-1], "ep")
     groups, half = router.shape[0], LANES // 2
     router = router.reshape(groups, parts, 8, 2, half).transpose(1, 4, 0, 3, 2)
     serve_router = router.reshape(parts * half, groups * 16)

time: 104 us -> 104 us (level)
  no operation moved by 1% of the time
where the time goes in v6:
time: 104 us; the launch traced here: 102 us
  waiting for transfers between devices  51.3 us (49%)
  starting transfers between devices  21 us (20%)
  Pallas kernels  14.6 us (14%)
  local copies, waits for them, and re-layouts  11.3 us (11%)
  other arithmetic  2.7 us (3%)
    all_to_all x2, waiting for transfers between devices, per_device(): lax.all_to_all(a, 'fsdp', split_axis=0, concat_axis=0, axis_index_groups=...  40.8 us
    all_to_all x2, starting transfers between devices, per_device(): lax.all_to_all(a, 'fsdp', split_axis=0, concat_axis=0, axis_index_groups=...  18.6 us
    ppermute x3, waiting for transfers between devices, gathered(): other = lax.ppermute(held, axis, [(i, i ^ bit) for i in range(n)])  10.5 us
    pallas_call x1, Pallas kernels, encode_rest(): pl.pallas_call(kernel, in_specs=[anywhere] * 4 + [vmem], out_specs=anywhe...  7.3 us
    pallas_call x1, Pallas kernels, decode(): pl.pallas_call(decode_kernel, in_specs=[vmem, vmem], out_specs=[anywhere]...  5.17 us
    another operation x1, local copies, waits for them, and re-layouts, per_device(): router = router.reshape(groups, parts, 8, 2, half).transpose(1, 4, 0, 3, 2)  3.17 us
    reshape x1, local copies, waits for them, and re-layouts, per_device(): serve_router = router.reshape(parts * half, groups * 16)  2.71 us
    transpose x1, local copies, waits for them, and re-layouts, per_device(): router = router.reshape(groups, parts, 8, 2, half).transpose(1, 4, 0, 3, 2)  2.47 us
  transfers between devices with their start and end apart: 5, of which 5 were waited for; matrix products, arithmetic and copies ran while one was open for 14% of the time, Pallas kernels for 7%

profile of v6, /device:TPU:22, one launch (start us, length us, event | category | flops | bytes accessed | tf_op | source)
XLA Modules:
  0.0 101.5 jit_solution(460202353088128301)
XLA Ops:
  0.6 2.1 %encode_first.1 = (bf16[32,32,128]{2,1,0:T(8,128)(2,1)}, f32[8,768]{1,0:T(8,128)}) custom-call(f32[16,64,768]{2,1,0:T(8,128)} %tg.3, bf16[16,64,768]{2,1,0:T(8,128)(2,1)} %og.3, f32[16,64,768]{2,1,0:T(8,128)} %tu.3, bf16[16,64,768]{2,1,0:T(8,128)(2,1)} %ou.3, f32[16,64]{1,0:T(8,128)} %bitcast.44, f32[1,64]{1,0:T(1,128)} %bitcast.45), custom_call_target="tpu_custom_call" | custom-call | flops 25000000 | bytes 900000 | tf_op jit(solution)/shard_map/encode_first/pallas_call | solution.py:65
  2.7 10.7 %all-to-all-start = ((bf16[32,32,128]{2,1,0:T(8,128)(2,1)}), bf16[32,32,128]{2,1,0:T(8,128)(2,1)S(1)}, u32[]{:S(2)}, u32[]{:S(2)}) async-start(bf16[32,32,128]{2,1,0:T(8,128)(2,1)} %get-tuple-element.11), calls=%async_computation | async-start | bytes 524288 | tf_op jit(solution)/shard_map/all_to_all | solution.py:323
  13.5 7.3 %encode_rest.1 = bf16[32,368,128]{2,1,0:T(8,128)(2,1)} custom-call(f32[16,64,768]{2,1,0:T(8,128)} %tg.3, bf16[16,64,768]{2,1,0:T(8,128)(2,1)} %og.3, f32[16,64,768]{2,1,0:T(8,128)} %tu.3, bf16[16,64,768]{2,1,0:T(8,128)(2,1)} %ou.3, f32[8,768]{1,0:T(8,128)} %get-tuple-element.12.before), custom_call_target="tpu_custom_call" | custom-call | flops 400000000 | bytes 11000000 | tf_op jit(solution)/shard_map/encode_rest/pallas_call | solution.py:134
  20.8 1.6 %all-to-all-done.first = bf16[32,32,128]{2,1,0:T(8,128)(2,1)S(1)} async-done(((bf16[32,32,128]{2,1,0:T(8,128)(2,1)}), bf16[32,32,128]{2,1,0:T(8,128)(2,1)S(1)}, u32[]{:S(2)}, u32[]{:S(2)}) %all-to-all-start) | async-done | bytes 262176 | tf_op jit(solution)/shard_map/all_to_all | solution.py:323
  22.3 7.9 %all-to-all-start.1 = ((bf16[32,368,128]{2,1,0:T(8,128)(2,1)}), bf16[32,368,128]{2,1,0:T(8,128)(2,1)S(1)}, u32[]{:S(2)}, u32[]{:S(2)}) async-start(bf16[32,368,128]{2,1,0:T(8,128)(2,1)} %encode_rest.1), calls=%async_computation.1 | async-start | bytes 6029312 | tf_op jit(solution)/shard_map/all_to_all | solution.py:323
  30.3 1.5 %collective-permute-start = (bf16[1,32,8,128]{3,2,1,0:T(8,128)(2,1)S(1)}, bf16[1,32,8,128]{3,2,1,0:T(8,128)(2,1)S(1)}, u32[]{:S(2)}, u32[]{:S(2)}) collective-permute-start(bf16[1,32,8,128]{3,2,1,0:T(8,128)(2,1)S(1)} %reverse_bitcast_fusion), channel_id=1, source_target_pairs={{0,128},{32,160},{64,192},{96,224},{128,0},{160,32},{192,64},{224,... | collective-permute-start | bytes 196616 | tf_op jit(solution)/shard_map/ppermute | solution.py:310
  31.8 4.4 %collective-permute-done = bf16[1,32,8,128]{3,2,1,0:T(8,128)(2,1)S(1)} collective-permute-done((bf16[1,32,8,128]{3,2,1,0:T(8,128)(2,1)S(1)}, bf16[1,32,8,128]{3,2,1,0:T(8,128)(2,1)S(1)}, u32[]{:S(2)}, u32[]{:S(2)}) %collective-permute-start) | collective-permute-done | bytes 65568 | tf_op jit(solution)/shard_map/ppermute | solution.py:310
  36.2 0.7 maximum_bitcast_fusion
  36.8 0.8 collective-permute-start.1
  37.7 4.5 %collective-permute-done.1 = bf16[2,32,8,128]{3,2,1,0:T(8,128)(2,1)} collective-permute-done((bf16[2,32,8,128]{3,2,1,0:T(8,128)(2,1)}, bf16[2,32,8,128]{3,2,1,0:T(8,128)(2,1)}, u32[]{:S(2)}, u32[]{:S(2)}) %collective-permute-start.1) | collective-permute-done | bytes 131104 | tf_op jit(solution)/shard_map/ppermute | solution.py:310
  42.1 0.9 select_bitcast_fusion.3
  43.1 0.1 collective-permute-start.2
  43.2 1.6 %collective-permute-done.2 = bf16[4,32,8,128]{3,2,1,0:T(8,128)(2,1)} collective-permute-done((bf16[4,32,8,128]{3,2,1,0:T(8,128)(2,1)S(1)}, bf16[4,32,8,128]{3,2,1,0:T(8,128)(2,1)}, u32[]{:S(2)}, u32[]{:S(2)}) %collective-permute-start.2) | collective-permute-done | bytes 262176 | tf_op jit(solution)/shard_map/ppermute | solution.py:310
  44.9 1.0 select_bitcast_fusion.1
  45.9 0.1 pad_maximum_fusion
  45.9 0.8 copy.12
  46.7 3.2 %reshape_reshape.3 = bf16[8,32,8,2,64]{4,3,2,1,0:T(2,128)(2,1)} reshape(bf16[4,2,32,8,128]{4,3,2,1,0:T(8,128)(2,1)} %copy.12) | data formatting | bytes 1048576 | tf_op jit(solution)/shard_map/reshape;reshape | solution.py:335
  49.9 2.5 %copy.13 = bf16[32,64,8,2,8]{1,0,4,3,2:T(8,128)(2,1)} copy(bf16[32,64,8,2,8]{1,3,4,0,2:T(2,128)(2,1)} %bitcast.42) | data formatting | bytes 1048576 | tf_op jit(solution)/shard_map/transpose | solution.py:335
  52.4 2.7 %reshape.29 = bf16[2048,128]{0,1:T(8,128)(2,1)} reshape(bf16[32,64,8,2,8]{1,0,4,3,2:T(8,128)(2,1)} %copy.13) | data formatting | bytes 1048576 | tf_op jit(solution)/shard_map/reshape | solution.py:336
  55.1 2.0 %copy.14 = bf16[2048,128]{1,0:T(8,128)(2,1)} copy(bf16[2048,128]{0,1:T(8,128)(2,1)} %reshape.29) | data formatting | bytes 1048576
  57.1 39.2 %all-to-all-done.1.rest = bf16[32,368,128]{2,1,0:T(8,128)(2,1)S(1)} async-done(((bf16[32,368,128]{2,1,0:T(8,128)(2,1)}), bf16[32,368,128]{2,1,0:T(8,128)(2,1)S(1)}, u32[]{:S(2)}, u32[]{:S(2)}) %all-to-all-start.1) | async-done | bytes 3014688 | tf_op jit(solution)/shard_map/all_to_all | solution.py:323
  96.4 5.2 %decode.1 = (bf16[384,2048]{1,0:T(8,128)(2,1)}, bf16[384,2048]{1,0:T(8,128)(2,1)}, f32[16,24]{1,0:T(8,128)}, f32[16,24]{1,0:T(8,128)}) custom-call(bf16[32,32,128]{2,1,0:T(8,128)(2,1)S(1)} %all-to-all-done.first, bf16[32,368,128]{2,1,0:T(8,128)(2,1)S(1)} %all-to-all-done.1.rest), custom_call_target="tpu_custom_call" | custom-call | flops 400000000 | bytes 6400000 | tf_op jit(solution)/shard_map/decode/pallas_call | solution.py:280
  (7 shorter events, 0.1 us)
Async XLA Ops:
  2.7 19.6 %all-to-all-start = ((bf16[32,32,128]{2,1,0:T(8,128)(2,1)}), bf16[32,32,128]{2,1,0:T(8,128)(2,1)S(1)}, u32[]{:S(2)}, u32[]{:S(2)}) async-start(bf16[32,32,128]{2,1,0:T(8,128)(2,1)} %get-tuple-element.11), calls=%async_computation | async-start | bytes 524288 | tf_op jit(solution)/shard_map/all_to_all | solution.py:323
  22.3 74.0 %all-to-all-start.1 = ((bf16[32,368,128]{2,1,0:T(8,128)(2,1)}), bf16[32,368,128]{2,1,0:T(8,128)(2,1)S(1)}, u32[]{:S(2)}, u32[]{:S(2)}) async-start(bf16[32,368,128]{2,1,0:T(8,128)(2,1)} %encode_rest.1), calls=%async_computation.1 | async-start | bytes 6029312 | tf_op jit(solution)/shard_map/all_to_all | solution.py:323
  30.3 5.9 %collective-permute-start = (bf16[1,32,8,128]{3,2,1,0:T(8,128)(2,1)S(1)}, bf16[1,32,8,128]{3,2,1,0:T(8,128)(2,1)S(1)}, u32[]{:S(2)}, u32[]{:S(2)}) collective-permute-start(bf16[1,32,8,128]{3,2,1,0:T(8,128)(2,1)S(1)} %reverse_bitcast_fusion), channel_id=1, source_target_pairs={{0,128},{32,160},{64,192},{96,224},{128,0},{160,32},{192,64},{224,... | collective-permute-start | bytes 196616 | tf_op jit(solution)/shard_map/ppermute | solution.py:310
  36.8 5.3 %collective-permute-start.1 = (bf16[2,32,8,128]{3,2,1,0:T(8,128)(2,1)}, bf16[2,32,8,128]{3,2,1,0:T(8,128)(2,1)}, u32[]{:S(2)}, u32[]{:S(2)}) collective-permute-start(bf16[2,32,8,128]{3,2,1,0:T(8,128)(2,1)} %maximum_bitcast_fusion), channel_id=1, source_target_pairs={{0,64},{32,96},{64,0},{96,32},{128,192},{160,224},{192,128},{224,1... | collective-permute-start | bytes 393224 | tf_op jit(solution)/shard_map/ppermute | solution.py:310
  43.1 1.8 %collective-permute-start.2 = (bf16[4,32,8,128]{3,2,1,0:T(8,128)(2,1)S(1)}, bf16[4,32,8,128]{3,2,1,0:T(8,128)(2,1)}, u32[]{:S(2)}, u32[]{:S(2)}) collective-permute-start(bf16[4,32,8,128]{3,2,1,0:T(8,128)(2,1)S(1)} %bitcast.43), channel_id=1, source_target_pairs={{0,32},{32,0},{64,96},{96,64},{128,160},{160,128},{192,224},{224,1... | collective-permute-start | bytes 786440 | tf_op jit(solution)/shard_map/ppermute | solution.py:310
